TPU v7x, 64 devices: a 2x2x8 block of a 4x4x8 slice. The times are simulated.
64 devices in a mesh: data: 4 (over x, y), cp: 16 (over z, core).
Axes of the slice: x: 2, y: 2, z: 8, core: 2. Of those that a mesh axis runs over, the one named last changes fastest.
The devices are a block of a 4x4x8 slice.
Arguments:
- q: bfloat16 [4, 4096, 8, 256], P('data', 'cp'), parts along dimension 0
- k: bfloat16 [4, 4096, 8, 256], P('data', 'cp'), parts along dimension 0
- v: bfloat16 [4, 4096, 8, 256], P('data', 'cp'), parts along dimension 0
- o: bfloat16 [4, 4096, 8, 256], P('data', 'cp'), parts along dimension 0
- lse: float32 [4, 8, 4096], P('data', None, 'cp'), parts along dimension 0
- do: bfloat16 [4, 4096, 8, 256], P('data', 'cp'), parts along dimension 0
Outputs:
- output 1: bfloat16 [4, 4096, 8, 256], P('data', 'cp'), parts along dimension 0
- output 2: bfloat16 [4, 4096, 8, 256], P('data', 'cp'), parts along dimension 0
- output 3: bfloat16 [4, 4096, 8, 256], P('data', 'cp'), parts along dimension 0
There are 4 independent parts. A program takes and returns all parts, laid end to end along the dimension named above; each array names one.
All inputs are finite; a program needn't handle non-finite values.
Results may differ from a plain program's by a relative error of at most 0.001.
Values are sent between devices in bfloat16 or wider.
A program may use at most 768 MiB of HBM per device.

v0:
```python
import jax
import jax.numpy as jnp
from jax import lax
from jax.sharding import PartitionSpec as P

F32 = jnp.float32
BF16 = jnp.bfloat16


def _pair(q, do, lse, delta, k, v, mask, scale):
    s = jnp.einsum('bqhd,bkhd->bhqk', q, k, preferred_element_type=F32) * scale
    p = jnp.exp(s - lse[..., None])
    if mask is not None:
        p = jnp.where(mask, p, 0.0)
    dv = jnp.einsum('bhqk,bqhd->bkhd', p.astype(BF16), do, preferred_element_type=F32)
    dp = jnp.einsum('bqhd,bkhd->bhqk', do, v, preferred_element_type=F32)
    ds = (p * (dp - delta[..., None])).astype(BF16)
    dq = jnp.einsum('bhqk,bkhd->bqhd', ds, k, preferred_element_type=F32) * scale
    dk = jnp.einsum('bhqk,bqhd->bkhd', ds, q, preferred_element_type=F32) * scale
    return dq, dk, dv


def _same(q, do, lse, delta, k, v):
    c = q.shape[1] // 2
    scale = q.shape[-1] ** -0.5
    tri = jnp.tril(jnp.ones((c, c), bool))
    full = jnp.concatenate([jnp.ones((c, c), bool), tri], axis=1)
    dq0, dk0, dv0 = _pair(q[:, :c], do[:, :c], lse[..., :c], delta[..., :c], k[:, :c], v[:, :c], tri, scale)
    dq1, dk1, dv1 = _pair(q[:, c:], do[:, c:], lse[..., c:], delta[..., c:], k, v, full, scale)
    return jnp.concatenate([dq0, dq1], axis=1), dk1.at[:, :c].add(dk0), dv1.at[:, :c].add(dv0)


def _second_queries(q, do, lse, delta, k, v):
    c = q.shape[1] // 2
    scale = q.shape[-1] ** -0.5
    dq, dk, dv = _pair(q[:, c:], do[:, c:], lse[..., c:], delta[..., c:], k, v, None, scale)
    return jnp.concatenate([jnp.zeros_like(dq), dq], axis=1), dk, dv


def _first_keys(q, do, lse, delta, k, v):
    c = q.shape[1] // 2
    scale = q.shape[-1] ** -0.5
    dq, dk, dv = _pair(q, do, lse, delta, k[:, :c], v[:, :c], None, scale)
    return dq, jnp.concatenate([dk, jnp.zeros_like(dk)], axis=1), jnp.concatenate([dv, jnp.zeros_like(dv)], axis=1)


def solution(mesh):
    n = mesh.shape['cp']
    nxt = [(j, (j + 1) % n) for j in range(n)]
    spec = P('data', 'cp', None, None)
    lspec = P('data', None, 'cp')

    def local(q, k, v, o, lse, do):
        i = lax.axis_index('cp')
        delta = jnp.einsum('bqhd,bqhd->bhq', do, o, preferred_element_type=F32)
        dq, dk, dv = _same(q, do, lse, delta, k, v)
        qt, dot, lt, deltat = q, do, lse, delta
        for r in range(1, n):
            qt, dot, lt, deltat, dq = (lax.ppermute(x, 'cp', nxt) for x in (qt, dot, lt, deltat, dq))
            src = (i - r) % n
            ddq, ddk, ddv = lax.cond(src < i, _second_queries, _first_keys, qt, dot, lt, deltat, k, v)
            dq = dq + ddq
            dk = dk + ddk
            dv = dv + ddv
        dq = lax.ppermute(dq, 'cp', nxt)
        return dq.astype(BF16), dk.astype(BF16), dv.astype(BF16)

    return jax.shard_map(local, mesh=mesh, in_specs=(spec, spec, spec, spec, lspec, spec),
                         out_specs=(spec, spec, spec), check_vma=False)
```

profile of v0, /device:TPU:22, one launch (start us, length us, event | category | flops | bytes accessed | tf_op | source)
XLA Modules:
  0.0 989.3 jit_solution(17970573403401619016)
XLA Ops:
  1.5 2.5 copy.69
  8.1 1.9 fusion.462
  15.9 2.3 collective-permute-start.1
  18.1 2.2 collective-permute-start.2
  20.4 48.6 %collective-permute-done.2 = f32[1,8,256]{2,1,0:T(8,128)S(1)} collective-permute-done((f32[1,8,256]{2,1,0:T(8,128)S(1)}, f32[1,8,256]{2,1,0:T(8,128)S(1)}, u32[]{:S(2)}, u32[]{:S(2)}) %collective-permute-start.2) | collective-permute-done | bytes 8224 | tf_op jit(solution)/shard_map/ppermute | solution.py:59
  69.0 9.4 conditional.15
  71.6 1.8 multiply_bitcast_fusion
  78.4 3.8 add.310
  82.4 49.0 %collective-permute-done.7 = f32[1,8,256]{2,1,0:T(8,128)S(1)} collective-permute-done((f32[1,8,256]{2,1,0:T(8,128)S(1)}, f32[1,8,256]{2,1,0:T(8,128)S(1)}, u32[]{:S(2)}, u32[]{:S(2)}) %collective-permute-start.7) | collective-permute-done | bytes 8224 | tf_op jit(solution)/shard_map/ppermute | solution.py:59
  131.5 12.1 %conditional.16 = (f32[1,256,8,256]{3,1,2,0:T(8,128)}, f32[1,256,8,256]{3,1,2,0:T(8,128)}, f32[1,256,8,256]{3,1,2,0:T(8,128)}) conditional(s32[]{:T(128)} %convert_element_type.313, (bf16[1,256,8,256]{3,1,2,0:T(8,128)(2,1)}, bf16[1,256,8,256]{3,2,1,0:T(8,128)(2,1)S(1)}, f32[1,8,256]{2,1,0:T(8,128)S(1)}, bf16[1,256,8,256]{3,1,2,0:T(8,128)(2,1)}, ...), branch_computations={%region_2.3_spmd, %region_3.4_spmd} | conditional | flops 673447936 | bytes 25182240 | solution.py:61
  135.3 1.8 multiply_bitcast_fusion.2
  143.7 3.8 add.312
  147.7 49.0 %collective-permute-done.12 = f32[1,8,256]{2,1,0:T(8,128)S(1)} collective-permute-done((f32[1,8,256]{2,1,0:T(8,128)S(1)}, f32[1,8,256]{2,1,0:T(8,128)S(1)}, u32[]{:S(2)}, u32[]{:S(2)}) %collective-permute-start.12) | collective-permute-done | bytes 8224 | tf_op jit(solution)/shard_map/ppermute | solution.py:59
  196.8 9.5 conditional.17
  199.4 1.8 multiply_bitcast_fusion.4
  206.3 3.8 add.314
  210.3 49.0 %collective-permute-done.17 = f32[1,8,256]{2,1,0:T(8,128)S(1)} collective-permute-done((f32[1,8,256]{2,1,0:T(8,128)S(1)}, f32[1,8,256]{2,1,0:T(8,128)S(1)}, u32[]{:S(2)}, u32[]{:S(2)}) %collective-permute-start.17) | collective-permute-done | bytes 8224 | tf_op jit(solution)/shard_map/ppermute | solution.py:59
  259.4 12.2 %conditional.18 = (f32[1,256,8,256]{3,1,2,0:T(8,128)}, f32[1,256,8,256]{3,1,2,0:T(8,128)}, f32[1,256,8,256]{3,1,2,0:T(8,128)}) conditional(s32[]{:T(128)} %convert_element_type.315, (bf16[1,256,8,256]{3,1,2,0:T(8,128)(2,1)}, bf16[1,256,8,256]{3,2,1,0:T(8,128)(2,1)S(1)}, f32[1,8,256]{2,1,0:T(8,128)S(1)}, bf16[1,256,8,256]{3,1,2,0:T(8,128)(2,1)}, ...), branch_computations={%region_6.7_spmd, %region_7.8_spmd} | conditional | flops 673447936 | bytes 25182240 | solution.py:61
  263.2 1.8 multiply_bitcast_fusion.6
  271.6 3.8 add.316
  275.6 49.0 %collective-permute-done.22 = f32[1,8,256]{2,1,0:T(8,128)S(1)} collective-permute-done((f32[1,8,256]{2,1,0:T(8,128)S(1)}, f32[1,8,256]{2,1,0:T(8,128)S(1)}, u32[]{:S(2)}, u32[]{:S(2)}) %collective-permute-start.22) | collective-permute-done | bytes 8224 | tf_op jit(solution)/shard_map/ppermute | solution.py:59
  324.7 9.4 conditional.19
  327.3 1.8 multiply_bitcast_fusion.8
  334.2 3.8 add.318
  338.2 49.0 %collective-permute-done.27 = f32[1,8,256]{2,1,0:T(8,128)S(1)} collective-permute-done((f32[1,8,256]{2,1,0:T(8,128)S(1)}, f32[1,8,256]{2,1,0:T(8,128)S(1)}, u32[]{:S(2)}, u32[]{:S(2)}) %collective-permute-start.27) | collective-permute-done | bytes 8224 | tf_op jit(solution)/shard_map/ppermute | solution.py:59
  387.3 12.0 %conditional.20 = (f32[1,256,8,256]{3,1,2,0:T(8,128)}, f32[1,256,8,256]{3,1,2,0:T(8,128)}, f32[1,256,8,256]{3,1,2,0:T(8,128)}) conditional(s32[]{:T(128)} %convert_element_type.317, (bf16[1,256,8,256]{3,1,2,0:T(8,128)(2,1)}, bf16[1,256,8,256]{3,2,1,0:T(8,128)(2,1)S(1)}, f32[1,8,256]{2,1,0:T(8,128)S(1)}, bf16[1,256,8,256]{3,1,2,0:T(8,128)(2,1)}, ...), branch_computations={%region_10.11_spmd, %region_11.12_spmd} | conditional | flops 673447936 | bytes 25182240 | solution.py:61
  391.1 1.8 multiply_bitcast_fusion.10
  399.3 3.8 add.320
  403.3 49.0 %collective-permute-done.32 = f32[1,8,256]{2,1,0:T(8,128)S(1)} collective-permute-done((f32[1,8,256]{2,1,0:T(8,128)S(1)}, f32[1,8,256]{2,1,0:T(8,128)S(1)}, u32[]{:S(2)}, u32[]{:S(2)}) %collective-permute-start.32) | collective-permute-done | bytes 8224 | tf_op jit(solution)/shard_map/ppermute | solution.py:59
  452.4 9.4 conditional.21
  461.9 3.8 add.322
  465.9 49.0 %collective-permute-done.37 = f32[1,8,256]{2,1,0:T(8,128)S(1)} collective-permute-done((f32[1,8,256]{2,1,0:T(8,128)S(1)}, f32[1,8,256]{2,1,0:T(8,128)S(1)}, u32[]{:S(2)}, u32[]{:S(2)}) %collective-permute-start.37) | collective-permute-done | bytes 8224 | tf_op jit(solution)/shard_map/ppermute | solution.py:59
  515.0 12.1 %conditional.22 = (f32[1,256,8,256]{3,1,2,0:T(8,128)}, f32[1,256,8,256]{3,1,2,0:T(8,128)}, f32[1,256,8,256]{3,1,2,0:T(8,128)}) conditional(s32[]{:T(128)} %convert_element_type.319, (bf16[1,256,8,256]{3,1,2,0:T(8,128)(2,1)}, bf16[1,256,8,256]{3,2,1,0:T(8,128)(2,1)S(1)}, f32[1,8,256]{2,1,0:T(8,128)S(1)}, bf16[1,256,8,256]{3,1,2,0:T(8,128)(2,1)}, ...), branch_computations={%region_14.15_spmd, %region_15.16_spmd} | conditional | flops 673447936 | bytes 25182240 | solution.py:61
  527.1 3.8 add.324
  531.0 49.0 %collective-permute-done.42 = f32[1,8,256]{2,1,0:T(8,128)S(1)} collective-permute-done((f32[1,8,256]{2,1,0:T(8,128)S(1)}, f32[1,8,256]{2,1,0:T(8,128)S(1)}, u32[]{:S(2)}, u32[]{:S(2)}) %collective-permute-start.42) | collective-permute-done | bytes 8224 | tf_op jit(solution)/shard_map/ppermute | solution.py:59
  580.2 9.4 conditional.23
  582.8 1.8 multiply_bitcast_fusion.16
  589.6 3.8 add.326
  593.6 49.0 %collective-permute-done.47 = f32[1,8,256]{2,1,0:T(8,128)S(1)} collective-permute-done((f32[1,8,256]{2,1,0:T(8,128)S(1)}, f32[1,8,256]{2,1,0:T(8,128)S(1)}, u32[]{:S(2)}, u32[]{:S(2)}) %collective-permute-start.47) | collective-permute-done | bytes 8224 | tf_op jit(solution)/shard_map/ppermute | solution.py:59
  642.7 12.3 %conditional.24 = (f32[1,256,8,256]{3,1,2,0:T(8,128)}, f32[1,256,8,256]{3,1,2,0:T(8,128)}, f32[1,256,8,256]{3,1,2,0:T(8,128)}) conditional(s32[]{:T(128)} %convert_element_type.321, (bf16[1,256,8,256]{3,1,2,0:T(8,128)(2,1)}, bf16[1,256,8,256]{3,2,1,0:T(8,128)(2,1)S(1)}, f32[1,8,256]{2,1,0:T(8,128)S(1)}, bf16[1,256,8,256]{3,1,2,0:T(8,128)(2,1)}, ...), branch_computations={%region_18.19_spmd, %region_19.20_spmd} | conditional | flops 673447936 | bytes 25182240 | solution.py:61
  655.0 3.8 add.328
  659.0 49.0 %collective-permute-done.52 = f32[1,8,256]{2,1,0:T(8,128)S(1)} collective-permute-done((f32[1,8,256]{2,1,0:T(8,128)S(1)}, f32[1,8,256]{2,1,0:T(8,128)S(1)}, u32[]{:S(2)}, u32[]{:S(2)}) %collective-permute-start.52) | collective-permute-done | bytes 8224 | tf_op jit(solution)/shard_map/ppermute | solution.py:59
  708.1 9.4 conditional.25
  717.5 3.8 add.330
  721.5 49.0 %collective-permute-done.57 = f32[1,8,256]{2,1,0:T(8,128)S(1)} collective-permute-done((f32[1,8,256]{2,1,0:T(8,128)S(1)}, f32[1,8,256]{2,1,0:T(8,128)S(1)}, u32[]{:S(2)}, u32[]{:S(2)}) %collective-permute-start.57) | collective-permute-done | bytes 8224 | tf_op jit(solution)/shard_map/ppermute | solution.py:59
  770.7 12.0 %conditional.26 = (f32[1,256,8,256]{3,1,2,0:T(8,128)}, f32[1,256,8,256]{3,1,2,0:T(8,128)}, f32[1,256,8,256]{3,1,2,0:T(8,128)}) conditional(s32[]{:T(128)} %convert_element_type.323, (bf16[1,256,8,256]{3,1,2,0:T(8,128)(2,1)}, bf16[1,256,8,256]{3,2,1,0:T(8,128)(2,1)S(1)}, f32[1,8,256]{2,1,0:T(8,128)S(1)}, bf16[1,256,8,256]{3,1,2,0:T(8,128)(2,1)}, ...), branch_computations={%region_22.23_spmd, %region_23.24_spmd} | conditional | flops 673447936 | bytes 25182240 | solution.py:61
  782.7 3.8 add.332
  786.7 49.0 %collective-permute-done.62 = f32[1,8,256]{2,1,0:T(8,128)S(1)} collective-permute-done((f32[1,8,256]{2,1,0:T(8,128)S(1)}, f32[1,8,256]{2,1,0:T(8,128)S(1)}, u32[]{:S(2)}, u32[]{:S(2)}) %collective-permute-start.62) | collective-permute-done | bytes 8224 | tf_op jit(solution)/shard_map/ppermute | solution.py:59
  835.8 9.4 conditional.27
  845.2 4.0 add.334
  849.4 37.7 %collective-permute-done.66 = bf16[1,256,8,256]{3,1,2,0:T(8,128)(2,1)} collective-permute-done((bf16[1,256,8,256]{3,1,2,0:T(8,128)(2,1)}, bf16[1,256,8,256]{3,1,2,0:T(8,128)(2,1)}, u32[]{:S(2)}, u32[]{:S(2)}) %collective-permute-start.66) | collective-permute-done | bytes 1048608 | tf_op jit(solution)/shard_map/ppermute | solution.py:59
  887.1 11.2 %collective-permute-done.68 = bf16[1,256,8,256]{3,1,2,0:T(8,128)(2,1)} collective-permute-done((bf16[1,256,8,256]{3,1,2,0:T(8,128)(2,1)S(1)}, bf16[1,256,8,256]{3,1,2,0:T(8,128)(2,1)}, u32[]{:S(2)}, u32[]{:S(2)}) %collective-permute-start.68) | collective-permute-done | bytes 1048608 | tf_op jit(solution)/shard_map/ppermute | solution.py:59
  898.3 2.9 fusion.471
  901.3 3.0 copy.503
  904.3 9.4 conditional.28
  915.7 4.0 add.336
  919.7 3.0 multiply_bitcast_fusion.30
  925.6 2.7 fusion.461
  928.3 18.1 %collective-permute-done.72 = f32[1,8,256]{2,1,0:T(8,128)S(1)} collective-permute-done((f32[1,8,256]{2,1,0:T(8,128)S(1)}, f32[1,8,256]{2,1,0:T(8,128)S(1)}, u32[]{:S(2)}, u32[]{:S(2)}) %collective-permute-start.72) | collective-permute-done | bytes 8224 | tf_op jit(solution)/shard_map/ppermute | solution.py:59
  946.6 9.5 conditional.29
  956.1 11.6 %add_convert_fusion.1 = bf16[1,256,8,256]{3,1,2,0:T(8,128)(2,1)S(1)} fusion(f32[1,256,8,256]{3,1,2,0:T(8,128)} %get-tuple-element.641, f32[1,256,8,256]{3,1,2,0:T(8,128)} %get-tuple-element.640, f32[1,256,8,256]{3,1,2,0:T(8,128)} %get-tuple-element.639, f32[1,256,8,256]{3,1,2,0:T(8,128)} %get-tuple-element.638, f32[1,256,8,256]{3,1,2,0:T(8,128)} %get-tuple-element.637, ...), kind=kLoop, calls=%fused_computation.664 | loop fusion | flops 8388608 | bytes 34603008 | tf_op jit(solution)/shard_map/convert_element_type | solution.py:66
  969.2 2.6 add.338
  972.7 10.5 %add_convert_fusion = bf16[1,256,8,256]{3,1,2,0:T(8,128)(2,1)S(1)} fusion(f32[1,256,8,256]{3,1,2,0:T(8,128)} %get-tuple-element.656, f32[1,256,8,256]{3,1,2,0:T(8,128)S(1)} %copy-done.8, f32[1,256,8,256]{3,1,2,0:T(8,128)} %get-tuple-element.654, f32[1,256,8,256]{3,1,2,0:T(8,128)} %get-tuple-element.653, f32[1,256,8,256]{3,1,2,0:T(8,128)} %get-tuple-element.652, ...), kind=kLoop, calls=%fused_computation.663 | loop fusion | flops 8388608 | bytes 34603008 | tf_op jit(solution)/shard_map/convert_element_type | solution.py:66
  984.8 2.5 collective-permute-done.75
  (320 shorter events, 166.7 us)
Async XLA Ops:
  15.9 62.6 %collective-permute-start = (f32[1,256,8,256]{3,1,2,0:T(8,128)}, f32[1,256,8,256]{3,1,2,0:T(8,128)}, u32[]{:S(2)}, u32[]{:S(2)}) collective-permute-start(f32[1,256,8,256]{3,1,2,0:T(8,128)} %pad_maximum_fusion), channel_id=1, source_target_pairs={{0,1},{1,2},{2,3},{3,4},{4,5},{5,6},{6,7},{7,8},{8,9},{9,10},{10,1... | collective-permute-start | bytes 6291464 | tf_op jit(solution)/shard_map/ppermute | solution.py:59
  15.9 53.2 %collective-permute-start.1 = (bf16[1,256,8,256]{3,1,2,0:T(8,128)(2,1)}, bf16[1,256,8,256]{3,1,2,0:T(8,128)(2,1)}, u32[]{:S(2)}, u32[]{:S(2)}) collective-permute-start(bf16[1,256,8,256]{3,1,2,0:T(8,128)(2,1)} %copy.69), channel_id=1, source_target_pairs={{0,1},{1,2},{2,3},{3,4},{4,5},{5,6},{6,7},{7,8},{8,9},{9,10},{10,1... | collective-permute-start | bytes 3145736 | tf_op jit(solution)/shard_map/ppermute | solution.py:59
  18.1 50.9 %collective-permute-start.3 = (bf16[1,256,8,256]{3,1,2,0:T(8,128)(2,1)}, bf16[1,256,8,256]{3,1,2,0:T(8,128)(2,1)S(1)}, u32[]{:S(2)}, u32[]{:S(2)}) collective-permute-start(bf16[1,256,8,256]{3,1,2,0:T(8,128)(2,1)} %copy.71), channel_id=1, source_target_pairs={{0,1},{1,2},{2,3},{3,4},{4,5},{5,6},{6,7},{7,8},{8,9},{9,10},{10,1... | collective-permute-start | bytes 3145736 | tf_op jit(solution)/shard_map/ppermute | solution.py:59
  18.1 50.8 %collective-permute-start.2 = (f32[1,8,256]{2,1,0:T(8,128)S(1)}, f32[1,8,256]{2,1,0:T(8,128)S(1)}, u32[]{:S(2)}, u32[]{:S(2)}) collective-permute-start(f32[1,8,256]{2,1,0:T(8,128)S(1)} %copy-done.19), channel_id=1, source_target_pairs={{0,1},{1,2},{2,3},{3,4},{4,5},{5,6},{6,7},{7,8},{8,9},{9,10},{10,1... | collective-permute-start | bytes 24584 | tf_op jit(solution)/shard_map/ppermute | solution.py:59
  82.2 61.5 %collective-permute-start.5 = (f32[1,256,8,256]{3,1,2,0:T(8,128)}, f32[1,256,8,256]{3,1,2,0:T(8,128)}, u32[]{:S(2)}, u32[]{:S(2)}) collective-permute-start(f32[1,256,8,256]{3,1,2,0:T(8,128)} %add.310), channel_id=1, source_target_pairs={{0,1},{1,2},{2,3},{3,4},{4,5},{5,6},{6,7},{7,8},{8,9},{9,10},{10,1... | collective-permute-start | bytes 6291464 | tf_op jit(solution)/shard_map/ppermute | solution.py:59
  82.2 49.3 %collective-permute-start.6 = (bf16[1,256,8,256]{3,1,2,0:T(8,128)(2,1)}, bf16[1,256,8,256]{3,1,2,0:T(8,128)(2,1)}, u32[]{:S(2)}, u32[]{:S(2)}) collective-permute-start(bf16[1,256,8,256]{3,1,2,0:T(8,128)(2,1)} %collective-permute-done.1), channel_id=1, source_target_pairs={{0,1},{1,2},{2,3},{3,4},{4,5},{5,6},{6,7},{7,8},{8,9},{9,10},{10,1... | collective-permute-start | bytes 3145736 | tf_op jit(solution)/shard_map/ppermute | solution.py:59
  82.2 49.3 %collective-permute-start.8 = (bf16[1,256,8,256]{3,1,2,0:T(8,128)(2,1)S(1)}, bf16[1,256,8,256]{3,1,2,0:T(8,128)(2,1)}, u32[]{:S(2)}, u32[]{:S(2)}) collective-permute-start(bf16[1,256,8,256]{3,1,2,0:T(8,128)(2,1)S(1)} %collective-permute-done.3), channel_id=1, source_target_pairs={{0,1},{1,2},{2,3},{3,4},{4,5},{5,6},{6,7},{7,8},{8,9},{9,10},{10,1... | collective-permute-start | bytes 3145736 | tf_op jit(solution)/shard_map/ppermute | solution.py:59
  82.2 49.2 %collective-permute-start.7 = (f32[1,8,256]{2,1,0:T(8,128)S(1)}, f32[1,8,256]{2,1,0:T(8,128)S(1)}, u32[]{:S(2)}, u32[]{:S(2)}) collective-permute-start(f32[1,8,256]{2,1,0:T(8,128)S(1)} %collective-permute-done.2), channel_id=1, source_target_pairs={{0,1},{1,2},{2,3},{3,4},{4,5},{5,6},{6,7},{7,8},{8,9},{9,10},{10,1... | collective-permute-start | bytes 24584 | tf_op jit(solution)/shard_map/ppermute | solution.py:59
  82.3 49.2 %collective-permute-start.9 = (f32[1,8,256]{2,1,0:T(8,128)S(1)}, f32[1,8,256]{2,1,0:T(8,128)S(1)}, u32[]{:S(2)}, u32[]{:S(2)}) collective-permute-start(f32[1,8,256]{2,1,0:T(8,128)S(1)} %collective-permute-done.4), channel_id=1, source_target_pairs={{0,1},{1,2},{2,3},{3,4},{4,5},{5,6},{6,7},{7,8},{8,9},{9,10},{10,1... | collective-permute-start | bytes 24584 | tf_op jit(solution)/shard_map/ppermute | solution.py:59
  147.5 58.8 %collective-permute-start.10 = (f32[1,256,8,256]{3,1,2,0:T(8,128)}, f32[1,256,8,256]{3,1,2,0:T(8,128)}, u32[]{:S(2)}, u32[]{:S(2)}) collective-permute-start(f32[1,256,8,256]{3,1,2,0:T(8,128)} %add.312), channel_id=1, source_target_pairs={{0,1},{1,2},{2,3},{3,4},{4,5},{5,6},{6,7},{7,8},{8,9},{9,10},{10,1... | collective-permute-start | bytes 6291464 | tf_op jit(solution)/shard_map/ppermute | solution.py:59
  147.5 49.3 %collective-permute-start.11 = (bf16[1,256,8,256]{3,1,2,0:T(8,128)(2,1)}, bf16[1,256,8,256]{3,1,2,0:T(8,128)(2,1)}, u32[]{:S(2)}, u32[]{:S(2)}) collective-permute-start(bf16[1,256,8,256]{3,1,2,0:T(8,128)(2,1)} %collective-permute-done.6), channel_id=1, source_target_pairs={{0,1},{1,2},{2,3},{3,4},{4,5},{5,6},{6,7},{7,8},{8,9},{9,10},{10,1... | collective-permute-start | bytes 3145736 | tf_op jit(solution)/shard_map/ppermute | solution.py:59
  147.5 49.3 %collective-permute-start.13 = (bf16[1,256,8,256]{3,1,2,0:T(8,128)(2,1)}, bf16[1,256,8,256]{3,1,2,0:T(8,128)(2,1)S(1)}, u32[]{:S(2)}, u32[]{:S(2)}) collective-permute-start(bf16[1,256,8,256]{3,1,2,0:T(8,128)(2,1)} %collective-permute-done.8), channel_id=1, source_target_pairs={{0,1},{1,2},{2,3},{3,4},{4,5},{5,6},{6,7},{7,8},{8,9},{9,10},{10,1... | collective-permute-start | bytes 3145736 | tf_op jit(solution)/shard_map/ppermute | solution.py:59
  147.5 49.2 %collective-permute-start.12 = (f32[1,8,256]{2,1,0:T(8,128)S(1)}, f32[1,8,256]{2,1,0:T(8,128)S(1)}, u32[]{:S(2)}, u32[]{:S(2)}) collective-permute-start(f32[1,8,256]{2,1,0:T(8,128)S(1)} %collective-permute-done.7), channel_id=1, source_target_pairs={{0,1},{1,2},{2,3},{3,4},{4,5},{5,6},{6,7},{7,8},{8,9},{9,10},{10,1... | collective-permute-start | bytes 24584 | tf_op jit(solution)/shard_map/ppermute | solution.py:59
  147.6 49.2 %collective-permute-start.14 = (f32[1,8,256]{2,1,0:T(8,128)S(1)}, f32[1,8,256]{2,1,0:T(8,128)S(1)}, u32[]{:S(2)}, u32[]{:S(2)}) collective-permute-start(f32[1,8,256]{2,1,0:T(8,128)S(1)} %collective-permute-done.9), channel_id=1, source_target_pairs={{0,1},{1,2},{2,3},{3,4},{4,5},{5,6},{6,7},{7,8},{8,9},{9,10},{10,1... | collective-permute-start | bytes 24584 | tf_op jit(solution)/shard_map/ppermute | solution.py:59
  210.1 61.6 %collective-permute-start.15 = (f32[1,256,8,256]{3,1,2,0:T(8,128)}, f32[1,256,8,256]{3,1,2,0:T(8,128)}, u32[]{:S(2)}, u32[]{:S(2)}) collective-permute-start(f32[1,256,8,256]{3,1,2,0:T(8,128)} %add.314), channel_id=1, source_target_pairs={{0,1},{1,2},{2,3},{3,4},{4,5},{5,6},{6,7},{7,8},{8,9},{9,10},{10,1... | collective-permute-start | bytes 6291464 | tf_op jit(solution)/shard_map/ppermute | solution.py:59
  210.1 49.3 %collective-permute-start.16 = (bf16[1,256,8,256]{3,1,2,0:T(8,128)(2,1)}, bf16[1,256,8,256]{3,1,2,0:T(8,128)(2,1)}, u32[]{:S(2)}, u32[]{:S(2)}) collective-permute-start(bf16[1,256,8,256]{3,1,2,0:T(8,128)(2,1)} %collective-permute-done.11), channel_id=1, source_target_pairs={{0,1},{1,2},{2,3},{3,4},{4,5},{5,6},{6,7},{7,8},{8,9},{9,10},{10,1... | collective-permute-start | bytes 3145736 | tf_op jit(solution)/shard_map/ppermute | solution.py:59
  210.1 49.3 %collective-permute-start.18 = (bf16[1,256,8,256]{3,1,2,0:T(8,128)(2,1)S(1)}, bf16[1,256,8,256]{3,1,2,0:T(8,128)(2,1)}, u32[]{:S(2)}, u32[]{:S(2)}) collective-permute-start(bf16[1,256,8,256]{3,1,2,0:T(8,128)(2,1)S(1)} %collective-permute-done.13), channel_id=1, source_target_pairs={{0,1},{1,2},{2,3},{3,4},{4,5},{5,6},{6,7},{7,8},{8,9},{9,10},{10,1... | collective-permute-start | bytes 3145736 | tf_op jit(solution)/shard_map/ppermute | solution.py:59
  210.2 49.2 %collective-permute-start.19 = (f32[1,8,256]{2,1,0:T(8,128)S(1)}, f32[1,8,256]{2,1,0:T(8,128)S(1)}, u32[]{:S(2)}, u32[]{:S(2)}) collective-permute-start(f32[1,8,256]{2,1,0:T(8,128)S(1)} %collective-permute-done.14), channel_id=1, source_target_pairs={{0,1},{1,2},{2,3},{3,4},{4,5},{5,6},{6,7},{7,8},{8,9},{9,10},{10,1... | collective-permute-start | bytes 24584 | tf_op jit(solution)/shard_map/ppermute | solution.py:59
  275.4 58.8 %collective-permute-start.20 = (f32[1,256,8,256]{3,1,2,0:T(8,128)}, f32[1,256,8,256]{3,1,2,0:T(8,128)}, u32[]{:S(2)}, u32[]{:S(2)}) collective-permute-start(f32[1,256,8,256]{3,1,2,0:T(8,128)} %add.316), channel_id=1, source_target_pairs={{0,1},{1,2},{2,3},{3,4},{4,5},{5,6},{6,7},{7,8},{8,9},{9,10},{10,1... | collective-permute-start | bytes 6291464 | tf_op jit(solution)/shard_map/ppermute | solution.py:59
  275.4 49.3 %collective-permute-start.21 = (bf16[1,256,8,256]{3,1,2,0:T(8,128)(2,1)}, bf16[1,256,8,256]{3,1,2,0:T(8,128)(2,1)}, u32[]{:S(2)}, u32[]{:S(2)}) collective-permute-start(bf16[1,256,8,256]{3,1,2,0:T(8,128)(2,1)} %collective-permute-done.16), channel_id=1, source_target_pairs={{0,1},{1,2},{2,3},{3,4},{4,5},{5,6},{6,7},{7,8},{8,9},{9,10},{10,1... | collective-permute-start | bytes 3145736 | tf_op jit(solution)/shard_map/ppermute | solution.py:59
  275.4 49.3 %collective-permute-start.23 = (bf16[1,256,8,256]{3,1,2,0:T(8,128)(2,1)}, bf16[1,256,8,256]{3,1,2,0:T(8,128)(2,1)S(1)}, u32[]{:S(2)}, u32[]{:S(2)}) collective-permute-start(bf16[1,256,8,256]{3,1,2,0:T(8,128)(2,1)} %collective-permute-done.18), channel_id=1, source_target_pairs={{0,1},{1,2},{2,3},{3,4},{4,5},{5,6},{6,7},{7,8},{8,9},{9,10},{10,1... | collective-permute-start | bytes 3145736 | tf_op jit(solution)/shard_map/ppermute | solution.py:59
  275.4 49.2 %collective-permute-start.22 = (f32[1,8,256]{2,1,0:T(8,128)S(1)}, f32[1,8,256]{2,1,0:T(8,128)S(1)}, u32[]{:S(2)}, u32[]{:S(2)}) collective-permute-start(f32[1,8,256]{2,1,0:T(8,128)S(1)} %collective-permute-done.17), channel_id=1, source_target_pairs={{0,1},{1,2},{2,3},{3,4},{4,5},{5,6},{6,7},{7,8},{8,9},{9,10},{10,1... | collective-permute-start | bytes 24584 | tf_op jit(solution)/shard_map/ppermute | solution.py:59
  275.5 49.2 %collective-permute-start.24 = (f32[1,8,256]{2,1,0:T(8,128)S(1)}, f32[1,8,256]{2,1,0:T(8,128)S(1)}, u32[]{:S(2)}, u32[]{:S(2)}) collective-permute-start(f32[1,8,256]{2,1,0:T(8,128)S(1)} %collective-permute-done.19), channel_id=1, source_target_pairs={{0,1},{1,2},{2,3},{3,4},{4,5},{5,6},{6,7},{7,8},{8,9},{9,10},{10,1... | collective-permute-start | bytes 24584 | tf_op jit(solution)/shard_map/ppermute | solution.py:59
  338.0 61.4 %collective-permute-start.25 = (f32[1,256,8,256]{3,1,2,0:T(8,128)}, f32[1,256,8,256]{3,1,2,0:T(8,128)}, u32[]{:S(2)}, u32[]{:S(2)}) collective-permute-start(f32[1,256,8,256]{3,1,2,0:T(8,128)} %add.318), channel_id=1, source_target_pairs={{0,1},{1,2},{2,3},{3,4},{4,5},{5,6},{6,7},{7,8},{8,9},{9,10},{10,1... | collective-permute-start | bytes 6291464 | tf_op jit(solution)/shard_map/ppermute | solution.py:59
  338.0 49.3 %collective-permute-start.26 = (bf16[1,256,8,256]{3,1,2,0:T(8,128)(2,1)}, bf16[1,256,8,256]{3,1,2,0:T(8,128)(2,1)}, u32[]{:S(2)}, u32[]{:S(2)}) collective-permute-start(bf16[1,256,8,256]{3,1,2,0:T(8,128)(2,1)} %collective-permute-done.21), channel_id=1, source_target_pairs={{0,1},{1,2},{2,3},{3,4},{4,5},{5,6},{6,7},{7,8},{8,9},{9,10},{10,1... | collective-permute-start | bytes 3145736 | tf_op jit(solution)/shard_map/ppermute | solution.py:59
  338.0 49.3 %collective-permute-start.28 = (bf16[1,256,8,256]{3,1,2,0:T(8,128)(2,1)S(1)}, bf16[1,256,8,256]{3,1,2,0:T(8,128)(2,1)}, u32[]{:S(2)}, u32[]{:S(2)}) collective-permute-start(bf16[1,256,8,256]{3,1,2,0:T(8,128)(2,1)S(1)} %collective-permute-done.23), channel_id=1, source_target_pairs={{0,1},{1,2},{2,3},{3,4},{4,5},{5,6},{6,7},{7,8},{8,9},{9,10},{10,1... | collective-permute-start | bytes 3145736 | tf_op jit(solution)/shard_map/ppermute | solution.py:59
  338.1 49.2 %collective-permute-start.29 = (f32[1,8,256]{2,1,0:T(8,128)S(1)}, f32[1,8,256]{2,1,0:T(8,128)S(1)}, u32[]{:S(2)}, u32[]{:S(2)}) collective-permute-start(f32[1,8,256]{2,1,0:T(8,128)S(1)} %collective-permute-done.24), channel_id=1, source_target_pairs={{0,1},{1,2},{2,3},{3,4},{4,5},{5,6},{6,7},{7,8},{8,9},{9,10},{10,1... | collective-permute-start | bytes 24584 | tf_op jit(solution)/shard_map/ppermute | solution.py:59
  403.1 58.7 %collective-permute-start.30 = (f32[1,256,8,256]{3,1,2,0:T(8,128)}, f32[1,256,8,256]{3,1,2,0:T(8,128)}, u32[]{:S(2)}, u32[]{:S(2)}) collective-permute-start(f32[1,256,8,256]{3,1,2,0:T(8,128)} %add.320), channel_id=1, source_target_pairs={{0,1},{1,2},{2,3},{3,4},{4,5},{5,6},{6,7},{7,8},{8,9},{9,10},{10,1... | collective-permute-start | bytes 6291464 | tf_op jit(solution)/shard_map/ppermute | solution.py:59
  403.1 49.3 %collective-permute-start.31 = (bf16[1,256,8,256]{3,1,2,0:T(8,128)(2,1)}, bf16[1,256,8,256]{3,1,2,0:T(8,128)(2,1)}, u32[]{:S(2)}, u32[]{:S(2)}) collective-permute-start(bf16[1,256,8,256]{3,1,2,0:T(8,128)(2,1)} %collective-permute-done.26), channel_id=1, source_target_pairs={{0,1},{1,2},{2,3},{3,4},{4,5},{5,6},{6,7},{7,8},{8,9},{9,10},{10,1... | collective-permute-start | bytes 3145736 | tf_op jit(solution)/shard_map/ppermute | solution.py:59
  403.1 49.3 %collective-permute-start.33 = (bf16[1,256,8,256]{3,1,2,0:T(8,128)(2,1)}, bf16[1,256,8,256]{3,1,2,0:T(8,128)(2,1)S(1)}, u32[]{:S(2)}, u32[]{:S(2)}) collective-permute-start(bf16[1,256,8,256]{3,1,2,0:T(8,128)(2,1)} %collective-permute-done.28), channel_id=1, source_target_pairs={{0,1},{1,2},{2,3},{3,4},{4,5},{5,6},{6,7},{7,8},{8,9},{9,10},{10,1... | collective-permute-start | bytes 3145736 | tf_op jit(solution)/shard_map/ppermute | solution.py:59
  403.1 49.2 %collective-permute-start.32 = (f32[1,8,256]{2,1,0:T(8,128)S(1)}, f32[1,8,256]{2,1,0:T(8,128)S(1)}, u32[]{:S(2)}, u32[]{:S(2)}) collective-permute-start(f32[1,8,256]{2,1,0:T(8,128)S(1)} %collective-permute-done.27), channel_id=1, source_target_pairs={{0,1},{1,2},{2,3},{3,4},{4,5},{5,6},{6,7},{7,8},{8,9},{9,10},{10,1... | collective-permute-start | bytes 24584 | tf_op jit(solution)/shard_map/ppermute | solution.py:59
  403.2 49.2 %collective-permute-start.34 = (f32[1,8,256]{2,1,0:T(8,128)S(1)}, f32[1,8,256]{2,1,0:T(8,128)S(1)}, u32[]{:S(2)}, u32[]{:S(2)}) collective-permute-start(f32[1,8,256]{2,1,0:T(8,128)S(1)} %collective-permute-done.29), channel_id=1, source_target_pairs={{0,1},{1,2},{2,3},{3,4},{4,5},{5,6},{6,7},{7,8},{8,9},{9,10},{10,1... | collective-permute-start | bytes 24584 | tf_op jit(solution)/shard_map/ppermute | solution.py:59
  465.7 61.4 %collective-permute-start.35 = (f32[1,256,8,256]{3,1,2,0:T(8,128)}, f32[1,256,8,256]{3,1,2,0:T(8,128)}, u32[]{:S(2)}, u32[]{:S(2)}) collective-permute-start(f32[1,256,8,256]{3,1,2,0:T(8,128)} %add.322), channel_id=1, source_target_pairs={{0,1},{1,2},{2,3},{3,4},{4,5},{5,6},{6,7},{7,8},{8,9},{9,10},{10,1... | collective-permute-start | bytes 6291464 | tf_op jit(solution)/shard_map/ppermute | solution.py:59
  465.7 49.3 %collective-permute-start.36 = (bf16[1,256,8,256]{3,1,2,0:T(8,128)(2,1)}, bf16[1,256,8,256]{3,1,2,0:T(8,128)(2,1)}, u32[]{:S(2)}, u32[]{:S(2)}) collective-permute-start(bf16[1,256,8,256]{3,1,2,0:T(8,128)(2,1)} %collective-permute-done.31), channel_id=1, source_target_pairs={{0,1},{1,2},{2,3},{3,4},{4,5},{5,6},{6,7},{7,8},{8,9},{9,10},{10,1... | collective-permute-start | bytes 3145736 | tf_op jit(solution)/shard_map/ppermute | solution.py:59
  465.7 49.3 %collective-permute-start.38 = (bf16[1,256,8,256]{3,1,2,0:T(8,128)(2,1)S(1)}, bf16[1,256,8,256]{3,1,2,0:T(8,128)(2,1)}, u32[]{:S(2)}, u32[]{:S(2)}) collective-permute-start(bf16[1,256,8,256]{3,1,2,0:T(8,128)(2,1)S(1)} %collective-permute-done.33), channel_id=1, source_target_pairs={{0,1},{1,2},{2,3},{3,4},{4,5},{5,6},{6,7},{7,8},{8,9},{9,10},{10,1... | collective-permute-start | bytes 3145736 | tf_op jit(solution)/shard_map/ppermute | solution.py:59
  465.8 49.2 %collective-permute-start.39 = (f32[1,8,256]{2,1,0:T(8,128)S(1)}, f32[1,8,256]{2,1,0:T(8,128)S(1)}, u32[]{:S(2)}, u32[]{:S(2)}) collective-permute-start(f32[1,8,256]{2,1,0:T(8,128)S(1)} %collective-permute-done.34), channel_id=1, source_target_pairs={{0,1},{1,2},{2,3},{3,4},{4,5},{5,6},{6,7},{7,8},{8,9},{9,10},{10,1... | collective-permute-start | bytes 24584 | tf_op jit(solution)/shard_map/ppermute | solution.py:59
  530.9 58.8 %collective-permute-start.40 = (f32[1,256,8,256]{3,1,2,0:T(8,128)}, f32[1,256,8,256]{3,1,2,0:T(8,128)}, u32[]{:S(2)}, u32[]{:S(2)}) collective-permute-start(f32[1,256,8,256]{3,1,2,0:T(8,128)} %add.324), channel_id=1, source_target_pairs={{0,1},{1,2},{2,3},{3,4},{4,5},{5,6},{6,7},{7,8},{8,9},{9,10},{10,1... | collective-permute-start | bytes 6291464 | tf_op jit(solution)/shard_map/ppermute | solution.py:59
  530.9 49.3 %collective-permute-start.41 = (bf16[1,256,8,256]{3,1,2,0:T(8,128)(2,1)}, bf16[1,256,8,256]{3,1,2,0:T(8,128)(2,1)}, u32[]{:S(2)}, u32[]{:S(2)}) collective-permute-start(bf16[1,256,8,256]{3,1,2,0:T(8,128)(2,1)} %collective-permute-done.36), channel_id=1, source_target_pairs={{0,1},{1,2},{2,3},{3,4},{4,5},{5,6},{6,7},{7,8},{8,9},{9,10},{10,1... | collective-permute-start | bytes 3145736 | tf_op jit(solution)/shard_map/ppermute | solution.py:59
  530.9 49.3 %collective-permute-start.43 = (bf16[1,256,8,256]{3,1,2,0:T(8,128)(2,1)}, bf16[1,256,8,256]{3,1,2,0:T(8,128)(2,1)S(1)}, u32[]{:S(2)}, u32[]{:S(2)}) collective-permute-start(bf16[1,256,8,256]{3,1,2,0:T(8,128)(2,1)} %collective-permute-done.38), channel_id=1, source_target_pairs={{0,1},{1,2},{2,3},{3,4},{4,5},{5,6},{6,7},{7,8},{8,9},{9,10},{10,1... | collective-permute-start | bytes 3145736 | tf_op jit(solution)/shard_map/ppermute | solution.py:59
  530.9 49.2 %collective-permute-start.42 = (f32[1,8,256]{2,1,0:T(8,128)S(1)}, f32[1,8,256]{2,1,0:T(8,128)S(1)}, u32[]{:S(2)}, u32[]{:S(2)}) collective-permute-start(f32[1,8,256]{2,1,0:T(8,128)S(1)} %collective-permute-done.37), channel_id=1, source_target_pairs={{0,1},{1,2},{2,3},{3,4},{4,5},{5,6},{6,7},{7,8},{8,9},{9,10},{10,1... | collective-permute-start | bytes 24584 | tf_op jit(solution)/shard_map/ppermute | solution.py:59
  531.0 49.2 %collective-permute-start.44 = (f32[1,8,256]{2,1,0:T(8,128)S(1)}, f32[1,8,256]{2,1,0:T(8,128)S(1)}, u32[]{:S(2)}, u32[]{:S(2)}) collective-permute-start(f32[1,8,256]{2,1,0:T(8,128)S(1)} %collective-permute-done.39), channel_id=1, source_target_pairs={{0,1},{1,2},{2,3},{3,4},{4,5},{5,6},{6,7},{7,8},{8,9},{9,10},{10,1... | collective-permute-start | bytes 24584 | tf_op jit(solution)/shard_map/ppermute | solution.py:59
  593.4 61.6 %collective-permute-start.45 = (f32[1,256,8,256]{3,1,2,0:T(8,128)}, f32[1,256,8,256]{3,1,2,0:T(8,128)}, u32[]{:S(2)}, u32[]{:S(2)}) collective-permute-start(f32[1,256,8,256]{3,1,2,0:T(8,128)} %add.326), channel_id=1, source_target_pairs={{0,1},{1,2},{2,3},{3,4},{4,5},{5,6},{6,7},{7,8},{8,9},{9,10},{10,1... | collective-permute-start | bytes 6291464 | tf_op jit(solution)/shard_map/ppermute | solution.py:59
  593.4 49.3 %collective-permute-start.46 = (bf16[1,256,8,256]{3,1,2,0:T(8,128)(2,1)}, bf16[1,256,8,256]{3,1,2,0:T(8,128)(2,1)}, u32[]{:S(2)}, u32[]{:S(2)}) collective-permute-start(bf16[1,256,8,256]{3,1,2,0:T(8,128)(2,1)} %collective-permute-done.41), channel_id=1, source_target_pairs={{0,1},{1,2},{2,3},{3,4},{4,5},{5,6},{6,7},{7,8},{8,9},{9,10},{10,1... | collective-permute-start | bytes 3145736 | tf_op jit(solution)/shard_map/ppermute | solution.py:59
  593.4 49.3 %collective-permute-start.48 = (bf16[1,256,8,256]{3,1,2,0:T(8,128)(2,1)S(1)}, bf16[1,256,8,256]{3,1,2,0:T(8,128)(2,1)}, u32[]{:S(2)}, u32[]{:S(2)}) collective-permute-start(bf16[1,256,8,256]{3,1,2,0:T(8,128)(2,1)S(1)} %collective-permute-done.43), channel_id=1, source_target_pairs={{0,1},{1,2},{2,3},{3,4},{4,5},{5,6},{6,7},{7,8},{8,9},{9,10},{10,1... | collective-permute-start | bytes 3145736 | tf_op jit(solution)/shard_map/ppermute | solution.py:59
  593.5 49.2 %collective-permute-start.49 = (f32[1,8,256]{2,1,0:T(8,128)S(1)}, f32[1,8,256]{2,1,0:T(8,128)S(1)}, u32[]{:S(2)}, u32[]{:S(2)}) collective-permute-start(f32[1,8,256]{2,1,0:T(8,128)S(1)} %collective-permute-done.44), channel_id=1, source_target_pairs={{0,1},{1,2},{2,3},{3,4},{4,5},{5,6},{6,7},{7,8},{8,9},{9,10},{10,1... | collective-permute-start | bytes 24584 | tf_op jit(solution)/shard_map/ppermute | solution.py:59
  658.8 58.8 %collective-permute-start.50 = (f32[1,256,8,256]{3,1,2,0:T(8,128)}, f32[1,256,8,256]{3,1,2,0:T(8,128)}, u32[]{:S(2)}, u32[]{:S(2)}) collective-permute-start(f32[1,256,8,256]{3,1,2,0:T(8,128)} %add.328), channel_id=1, source_target_pairs={{0,1},{1,2},{2,3},{3,4},{4,5},{5,6},{6,7},{7,8},{8,9},{9,10},{10,1... | collective-permute-start | bytes 6291464 | tf_op jit(solution)/shard_map/ppermute | solution.py:59
  658.8 49.3 %collective-permute-start.51 = (bf16[1,256,8,256]{3,1,2,0:T(8,128)(2,1)}, bf16[1,256,8,256]{3,1,2,0:T(8,128)(2,1)}, u32[]{:S(2)}, u32[]{:S(2)}) collective-permute-start(bf16[1,256,8,256]{3,1,2,0:T(8,128)(2,1)} %collective-permute-done.46), channel_id=1, source_target_pairs={{0,1},{1,2},{2,3},{3,4},{4,5},{5,6},{6,7},{7,8},{8,9},{9,10},{10,1... | collective-permute-start | bytes 3145736 | tf_op jit(solution)/shard_map/ppermute | solution.py:59
  658.8 49.3 %collective-permute-start.53 = (bf16[1,256,8,256]{3,1,2,0:T(8,128)(2,1)}, bf16[1,256,8,256]{3,1,2,0:T(8,128)(2,1)S(1)}, u32[]{:S(2)}, u32[]{:S(2)}) collective-permute-start(bf16[1,256,8,256]{3,1,2,0:T(8,128)(2,1)} %collective-permute-done.48), channel_id=1, source_target_pairs={{0,1},{1,2},{2,3},{3,4},{4,5},{5,6},{6,7},{7,8},{8,9},{9,10},{10,1... | collective-permute-start | bytes 3145736 | tf_op jit(solution)/shard_map/ppermute | solution.py:59
  658.8 49.2 %collective-permute-start.52 = (f32[1,8,256]{2,1,0:T(8,128)S(1)}, f32[1,8,256]{2,1,0:T(8,128)S(1)}, u32[]{:S(2)}, u32[]{:S(2)}) collective-permute-start(f32[1,8,256]{2,1,0:T(8,128)S(1)} %collective-permute-done.47), channel_id=1, source_target_pairs={{0,1},{1,2},{2,3},{3,4},{4,5},{5,6},{6,7},{7,8},{8,9},{9,10},{10,1... | collective-permute-start | bytes 24584 | tf_op jit(solution)/shard_map/ppermute | solution.py:59
  658.9 49.2 %collective-permute-start.54 = (f32[1,8,256]{2,1,0:T(8,128)S(1)}, f32[1,8,256]{2,1,0:T(8,128)S(1)}, u32[]{:S(2)}, u32[]{:S(2)}) collective-permute-start(f32[1,8,256]{2,1,0:T(8,128)S(1)} %collective-permute-done.49), channel_id=1, source_target_pairs={{0,1},{1,2},{2,3},{3,4},{4,5},{5,6},{6,7},{7,8},{8,9},{9,10},{10,1... | collective-permute-start | bytes 24584 | tf_op jit(solution)/shard_map/ppermute | solution.py:59
  721.3 61.3 %collective-permute-start.55 = (f32[1,256,8,256]{3,1,2,0:T(8,128)}, f32[1,256,8,256]{3,1,2,0:T(8,128)}, u32[]{:S(2)}, u32[]{:S(2)}) collective-permute-start(f32[1,256,8,256]{3,1,2,0:T(8,128)} %add.330), channel_id=1, source_target_pairs={{0,1},{1,2},{2,3},{3,4},{4,5},{5,6},{6,7},{7,8},{8,9},{9,10},{10,1... | collective-permute-start | bytes 6291464 | tf_op jit(solution)/shard_map/ppermute | solution.py:59
  721.3 49.3 %collective-permute-start.56 = (bf16[1,256,8,256]{3,1,2,0:T(8,128)(2,1)}, bf16[1,256,8,256]{3,1,2,0:T(8,128)(2,1)}, u32[]{:S(2)}, u32[]{:S(2)}) collective-permute-start(bf16[1,256,8,256]{3,1,2,0:T(8,128)(2,1)} %collective-permute-done.51), channel_id=1, source_target_pairs={{0,1},{1,2},{2,3},{3,4},{4,5},{5,6},{6,7},{7,8},{8,9},{9,10},{10,1... | collective-permute-start | bytes 3145736 | tf_op jit(solution)/shard_map/ppermute | solution.py:59
  721.3 49.3 %collective-permute-start.58 = (bf16[1,256,8,256]{3,1,2,0:T(8,128)(2,1)S(1)}, bf16[1,256,8,256]{3,1,2,0:T(8,128)(2,1)}, u32[]{:S(2)}, u32[]{:S(2)}) collective-permute-start(bf16[1,256,8,256]{3,1,2,0:T(8,128)(2,1)S(1)} %collective-permute-done.53), channel_id=1, source_target_pairs={{0,1},{1,2},{2,3},{3,4},{4,5},{5,6},{6,7},{7,8},{8,9},{9,10},{10,1... | collective-permute-start | bytes 3145736 | tf_op jit(solution)/shard_map/ppermute | solution.py:59
  721.4 49.2 %collective-permute-start.59 = (f32[1,8,256]{2,1,0:T(8,128)S(1)}, f32[1,8,256]{2,1,0:T(8,128)S(1)}, u32[]{:S(2)}, u32[]{:S(2)}) collective-permute-start(f32[1,8,256]{2,1,0:T(8,128)S(1)} %collective-permute-done.54), channel_id=1, source_target_pairs={{0,1},{1,2},{2,3},{3,4},{4,5},{5,6},{6,7},{7,8},{8,9},{9,10},{10,1... | collective-permute-start | bytes 24584 | tf_op jit(solution)/shard_map/ppermute | solution.py:59
  786.5 58.8 %collective-permute-start.60 = (f32[1,256,8,256]{3,1,2,0:T(8,128)}, f32[1,256,8,256]{3,1,2,0:T(8,128)}, u32[]{:S(2)}, u32[]{:S(2)}) collective-permute-start(f32[1,256,8,256]{3,1,2,0:T(8,128)} %add.332), channel_id=1, source_target_pairs={{0,1},{1,2},{2,3},{3,4},{4,5},{5,6},{6,7},{7,8},{8,9},{9,10},{10,1... | collective-permute-start | bytes 6291464 | tf_op jit(solution)/shard_map/ppermute | solution.py:59
  786.5 49.3 %collective-permute-start.61 = (bf16[1,256,8,256]{3,1,2,0:T(8,128)(2,1)}, bf16[1,256,8,256]{3,1,2,0:T(8,128)(2,1)}, u32[]{:S(2)}, u32[]{:S(2)}) collective-permute-start(bf16[1,256,8,256]{3,1,2,0:T(8,128)(2,1)} %collective-permute-done.56), channel_id=1, source_target_pairs={{0,1},{1,2},{2,3},{3,4},{4,5},{5,6},{6,7},{7,8},{8,9},{9,10},{10,1... | collective-permute-start | bytes 3145736 | tf_op jit(solution)/shard_map/ppermute | solution.py:59
  786.5 49.3 %collective-permute-start.63 = (bf16[1,256,8,256]{3,1,2,0:T(8,128)(2,1)}, bf16[1,256,8,256]{3,1,2,0:T(8,128)(2,1)S(1)}, u32[]{:S(2)}, u32[]{:S(2)}) collective-permute-start(bf16[1,256,8,256]{3,1,2,0:T(8,128)(2,1)} %collective-permute-done.58), channel_id=1, source_target_pairs={{0,1},{1,2},{2,3},{3,4},{4,5},{5,6},{6,7},{7,8},{8,9},{9,10},{10,1... | collective-permute-start | bytes 3145736 | tf_op jit(solution)/shard_map/ppermute | solution.py:59
  786.5 49.2 %collective-permute-start.62 = (f32[1,8,256]{2,1,0:T(8,128)S(1)}, f32[1,8,256]{2,1,0:T(8,128)S(1)}, u32[]{:S(2)}, u32[]{:S(2)}) collective-permute-start(f32[1,8,256]{2,1,0:T(8,128)S(1)} %collective-permute-done.57), channel_id=1, source_target_pairs={{0,1},{1,2},{2,3},{3,4},{4,5},{5,6},{6,7},{7,8},{8,9},{9,10},{10,1... | collective-permute-start | bytes 24584 | tf_op jit(solution)/shard_map/ppermute | solution.py:59
  786.6 49.2 %collective-permute-start.64 = (f32[1,8,256]{2,1,0:T(8,128)S(1)}, f32[1,8,256]{2,1,0:T(8,128)S(1)}, u32[]{:S(2)}, u32[]{:S(2)}) collective-permute-start(f32[1,8,256]{2,1,0:T(8,128)S(1)} %collective-permute-done.59), channel_id=1, source_target_pairs={{0,1},{1,2},{2,3},{3,4},{4,5},{5,6},{6,7},{7,8},{8,9},{9,10},{10,1... | collective-permute-start | bytes 24584 | tf_op jit(solution)/shard_map/ppermute | solution.py:59
  849.2 64.5 %collective-permute-start.65 = (f32[1,256,8,256]{3,1,2,0:T(8,128)}, f32[1,256,8,256]{3,1,2,0:T(8,128)}, u32[]{:S(2)}, u32[]{:S(2)}) collective-permute-start(f32[1,256,8,256]{3,1,2,0:T(8,128)} %add.334), channel_id=1, source_target_pairs={{0,1},{1,2},{2,3},{3,4},{4,5},{5,6},{6,7},{7,8},{8,9},{9,10},{10,1... | collective-permute-start | bytes 6291464 | tf_op jit(solution)/shard_map/ppermute | solution.py:59
  849.2 55.1 %collective-permute-start.67 = (f32[1,8,256]{2,1,0:T(8,128)S(1)}, f32[1,8,256]{2,1,0:T(8,128)S(1)}, u32[]{:S(2)}, u32[]{:S(2)}) collective-permute-start(f32[1,8,256]{2,1,0:T(8,128)S(1)} %collective-permute-done.62), channel_id=1, source_target_pairs={{0,1},{1,2},{2,3},{3,4},{4,5},{5,6},{6,7},{7,8},{8,9},{9,10},{10,1... | collective-permute-start | bytes 24584 | tf_op jit(solution)/shard_map/ppermute | solution.py:59
  849.3 55.0 %collective-permute-start.69 = (f32[1,8,256]{2,1,0:T(8,128)S(1)}, f32[1,8,256]{2,1,0:T(8,128)S(1)}, u32[]{:S(2)}, u32[]{:S(2)}) collective-permute-start(f32[1,8,256]{2,1,0:T(8,128)S(1)} %collective-permute-done.64), channel_id=1, source_target_pairs={{0,1},{1,2},{2,3},{3,4},{4,5},{5,6},{6,7},{7,8},{8,9},{9,10},{10,1... | collective-permute-start | bytes 24584 | tf_op jit(solution)/shard_map/ppermute | solution.py:59
  887.1 59.4 %collective-permute-start.71 = (bf16[1,256,8,256]{3,1,2,0:T(8,128)(2,1)}, bf16[1,256,8,256]{3,1,2,0:T(8,128)(2,1)}, u32[]{:S(2)}, u32[]{:S(2)}) collective-permute-start(bf16[1,256,8,256]{3,1,2,0:T(8,128)(2,1)} %collective-permute-done.66), channel_id=1, source_target_pairs={{0,1},{1,2},{2,3},{3,4},{4,5},{5,6},{6,7},{7,8},{8,9},{9,10},{10,1... | collective-permute-start | bytes 3145736 | tf_op jit(solution)/shard_map/ppermute | solution.py:59
  919.7 49.5 %collective-permute-start.70 = (f32[1,256,8,256]{3,1,2,0:T(8,128)}, f32[1,256,8,256]{3,1,2,0:T(8,128)}, u32[]{:S(2)}, u32[]{:S(2)}) collective-permute-start(f32[1,256,8,256]{3,1,2,0:T(8,128)} %add.336), channel_id=1, source_target_pairs={{0,1},{1,2},{2,3},{3,4},{4,5},{5,6},{6,7},{7,8},{8,9},{9,10},{10,1... | collective-permute-start | bytes 6291464 | tf_op jit(solution)/shard_map/ppermute | solution.py:59
  (32 other events, 591.4 us)
where the time goes:
time: 1000 us; the launch traced here: 989 us
  waiting for transfers between devices  708 us (71%)
  matrix products  121 us (12%)
  other arithmetic  80 us (8%)
  local copies, waits for them, and re-layouts  69 us (7%)
    ppermute x75, waiting for transfers between devices, local(): lax.ppermute(x, 'cp', nxt)  705 us
    add x15, other arithmetic, local(): dq = dq + ddq  56 us
    dot_general x17, matrix products, _pair(): jnp.einsum('bhqk,bqhd->bkhd', ds, q, preferred_element_type=F32) * scale  29.4 us
    dot_general x17, matrix products, _pair(): s = jnp.einsum('bqhd,bkhd->bhqk', q, k, preferred_element_type=F32) * scale  28.1 us
    dot_general x17, matrix products, _pair(): jnp.einsum('bhqk,bkhd->bqhd', ds, k, preferred_element_type=F32) * scale  26.4 us
    concatenate x15, local copies, waits for them, and re-layouts, _first_keys(): jnp.concatenate([dk, jnp.zeros_like(dk)], axis=1)  23 us
    convert_element_type x2, other arithmetic, local(): return (dq.astype(BF16), dk.astype(BF16), dv.astype(BF16))  22.1 us
    concatenate x15, local copies, waits for them, and re-layouts, _first_keys(): jnp.concatenate([dv, jnp.zeros_like(dv)], axis=1)  21.8 us
  transfers between devices with their start and end apart: 76, of which 31 were waited for; matrix products, arithmetic and copies ran while one was open for 20% of the time, Pallas kernels for 0%

commit v1 on v0

v1 whole, which is shorter than its diff:
```python
import functools

import jax
import jax.numpy as jnp
from jax import lax
from jax.experimental import pallas as pl
from jax.experimental.pallas import tpu as pltpu
from jax.sharding import PartitionSpec as P

F32 = jnp.float32
BF16 = jnp.bfloat16
MESH = pl.DeviceIdType.MESH
EARLY, LATE = 0, 1
K, V, Q, DO, O = range(5)


def _dot(a, b):
    return jnp.dot(a, b, preferred_element_type=F32)


def _dot_nt(a, b):
    return lax.dot_general(a, b, (((1,), (1,)), ((), ())), preferred_element_type=F32)


def _kernel(n, q_h, k_h, v_h, o_h, do_h, lse_h, dq_h, dk_h, dv_h,
            raw, lse_v, wide, send, ldsend, kv, qd, ld, kt, dqt, dqx, dkv, outs, outr, outv,
            load_sem, lse_sem, store_sem, kv_s, kv_r, qd_s, qd_r, ld_s, ld_r,
            fw_s, fw_r, fl_s, fl_r, dx_s, dx_r, og_s, og_r, oq_s, oq_r):
    chips = n // 2
    tokens, heads, dim = raw.shape[1:]
    c = tokens // 2
    lanes = wide.shape[-1]
    scale = dim ** -0.5
    me = lax.axis_index('cp')
    z = me // 2
    core = me % 2
    sib = me + 1 - 2 * core
    around = list(range(chips // 2, 0, -1))
    around = [d for k in around for d in ([k] if 2 * k == chips else [k, chips - k])]

    def peer(chip):
        return {'cp': 2 * chip + core}

    barrier = pltpu.get_barrier_semaphore()
    for d in range(1, chips):
        pl.semaphore_signal(barrier, inc=1, device_id=peer((z + d) % chips), device_id_type=MESH)
    pl.semaphore_signal(barrier, inc=1, device_id={'cp': sib}, device_id_type=MESH)

    hbm = {K: k_h, V: v_h, Q: q_h, DO: do_h, O: o_h}

    def load(t, half):
        rows = pl.ds(half * c, c)
        return pltpu.make_async_copy(hbm[t].at[rows], raw.at[t, rows], load_sem.at[t, half])

    for half in (LATE, EARLY):
        for t in (K, V, Q, DO, O):
            load(t, half).start()
    lse_load = pltpu.make_async_copy(lse_h, lse_v, lse_sem)
    lse_load.start()

    def spread(x):
        for l in range(dim // lanes):
            wide[l] = x[:, :, l * lanes:(l + 1) * lanes].reshape(c * heads, lanes)

    def head_rows(h):
        return pl.ds(h, c, stride=heads)

    def relayout(t, half, wait=True):
        if wait:
            load(t, half).wait()
        spread(raw[t, pl.ds(half * c, c)].astype(F32))
        for h in range(heads):
            for l in range(dim // lanes):
                send[half, t, h, :, pl.ds(l * lanes, lanes)] = wide[l, head_rows(h), :].astype(BF16)

    def copy_kv(half, d, slot):
        head = (z + d) % chips
        src, dst = send.at[half, pl.ds(K, 2), head], kv.at[half, :, slot]
        if d == 0:
            return pltpu.make_async_copy(src, dst, kv_r.at[half, slot])
        return pltpu.make_async_remote_copy(src, dst, kv_s.at[half, d], kv_r.at[half, slot],
                                            device_id=peer(head), device_id_type=MESH)

    def copy_qd(half, d, slot):
        head = (z + d) % chips
        src, dst = send.at[half, pl.ds(Q, 2), head], qd.at[half, :, 2 * slot + core]
        if d == 0:
            return pltpu.make_async_copy(src, dst, qd_r.at[half, slot])
        return pltpu.make_async_remote_copy(src, dst, qd_s.at[half, d], qd_r.at[half, slot],
                                            device_id=peer(head), device_id_type=MESH)

    def copy_ld(d, slot):
        head = (z + d) % chips
        src, dst = ldsend.at[head], ld.at[2 * slot + core]
        if d == 0:
            return pltpu.make_async_copy(src, dst, ld_r.at[slot])
        return pltpu.make_async_remote_copy(src, dst, ld_s.at[d], ld_r.at[slot],
                                            device_id=peer(head), device_id_type=MESH)

    def forward_qd(half, slot, parity):
        ref = qd.at[half, :, 2 * slot + parity]
        return pltpu.make_async_remote_copy(ref, ref, fw_s.at[half, slot], fw_r.at[half, slot],
                                            device_id={'cp': sib}, device_id_type=MESH)

    def forward_ld(slot, parity):
        ref = ld.at[2 * slot + parity]
        return pltpu.make_async_remote_copy(ref, ref, fl_s.at[slot], fl_r.at[slot],
                                            device_id={'cp': sib}, device_id_type=MESH)

    def exchange_dq(half):
        return pltpu.make_async_remote_copy(dqt.at[half, :, 1 - core], dqx.at[half], dx_s.at[half], dx_r.at[half],
                                            device_id={'cp': sib}, device_id_type=MESH)

    def copy_dkv(half, d, slot):
        chip = (z + d) % chips
        src, dst = outs.at[half, pl.ds(0, 2), chip], outr.at[half, pl.ds(0, 2), slot]
        if d == 0:
            return pltpu.make_async_copy(src, dst, og_r.at[half, slot])
        return pltpu.make_async_remote_copy(src, dst, og_s.at[half, d], og_r.at[half, slot],
                                            device_id=peer(chip), device_id_type=MESH)

    def copy_dq(half, d, slot):
        chip = (z + d) % chips
        src, dst = outs.at[half, 2, chip], outr.at[half, 2, slot]
        if d == 0:
            return pltpu.make_async_copy(src, dst, oq_r.at[half, slot])
        return pltpu.make_async_remote_copy(src, dst, oq_s.at[half, d], oq_r.at[half, slot],
                                            device_id=peer(chip), device_id_type=MESH)

    def start_all(make):
        for d in around + [0]:
            make(d, z).start()

    def wait_from(make, d):
        if d == 0:
            make(0, z).wait()
        else:
            make(d, (z - d + chips) % chips).wait_recv()

    def wait_sent(make):
        for d in around:
            make(d, z).wait_send()

    relayout(K, LATE)
    relayout(V, LATE)
    pl.semaphore_wait(barrier, chips)
    start_all(functools.partial(copy_kv, LATE))
    relayout(Q, LATE)
    relayout(DO, LATE)
    start_all(functools.partial(copy_qd, LATE))
    lse_load.wait()
    for half in (LATE, EARLY):
        load(O, half).wait()
        if half == EARLY:
            load(DO, half).wait()
        rows = pl.ds(half * c, c)
        spread(raw[DO, rows].astype(F32) * raw[O, rows].astype(F32))
        for h in range(heads):
            prod = sum(wide[l, head_rows(h), :] for l in range(dim // lanes))
            ldsend[h, pl.ds(2 + half, 1), :] = jnp.sum(prod.T, axis=0, keepdims=True)
            ldsend[h, pl.ds(half, 1), :] = lse_v[pl.ds(h, 1), pl.ds(half * c, c)]
    start_all(copy_ld)

    relayout(K, EARLY)
    relayout(V, EARLY)
    start_all(functools.partial(copy_kv, EARLY))
    relayout(Q, EARLY)
    relayout(DO, EARLY, wait=False)
    start_all(functools.partial(copy_qd, EARLY))

    def clear(s, carry):
        for half in range(2):
            for p in range(2):
                dqt[half, s, p] = jnp.zeros((dim, c), F32)
                dkv[half, p, s] = jnp.zeros((c, dim), F32)
        return carry

    lax.fori_loop(0, chips, clear, 0)

    def tile(kh, qh, i, j, width, masked):
        k = kv[kh, 0, pl.ds(2 * i, 2)].reshape(2 * c, dim)
        v = kv[kh, 1, pl.ds(2 * i, 2)].reshape(2 * c, dim)
        first = width * j
        q = qd[qh, 0, pl.ds(first, width)].reshape(width * c, dim)
        do = qd[qh, 1, pl.ds(first, width)].reshape(width * c, dim)
        lse = jnp.concatenate([ld[first + w, pl.ds(qh, 1), :] for w in range(width)], axis=1)
        delta = jnp.concatenate([ld[first + w, pl.ds(2 + qh, 1), :] for w in range(width)], axis=1)
        p = jnp.exp(_dot_nt(k, q) * scale - lse)
        if masked:
            sign = 1 if kh == EARLY else -1
            row = lax.broadcasted_iota(jnp.int32, (2 * c, width * c), 0)
            col = lax.broadcasted_iota(jnp.int32, (2 * c, width * c), 1)
            kpos = jnp.where(row >= c, row - c + sign * 2 * c, row) + sign * (4 * i + core) * c
            qpos = jnp.where(col >= c, col - c + sign * c, col) + sign * first * c
            p = jnp.where(qpos >= kpos, p, 0.0)
        rows = pl.ds(2 * i, 2)
        dkv[kh, 1, rows] += _dot(p.astype(BF16), do).reshape(2, c, dim)
        ds = (p * (_dot_nt(v, do) - delta)).astype(BF16)
        dkv[kh, 0, rows] += _dot(ds, q).reshape(2, c, dim)
        dq = _dot(kt[...], ds)
        for w in range(width):
            dqt[qh, width // 2 * j + w // 2, w % 2] += dq[:, w * c:(w + 1) * c]

    def sweep(kh, qh, lo, hi, width, masked):
        def outer(i, carry):
            kt[...] = kv[kh, 0, pl.ds(2 * i, 2)].reshape(2 * c, dim).T

            def inner(j, carry):
                tile(kh, qh, i, j, width, masked)
                return carry

            lax.fori_loop(lo(i), hi(i), inner, 0)
            return carry

        lax.fori_loop(0, chips // 2, outer, 0)

    def receive_qd(half):
        for d in [0] + around[::-1]:
            wait_from(functools.partial(copy_qd, half), d)
            forward_qd(half, (z - d + chips) % chips, core).start()

    def receive_forwarded(half):
        for s in range(chips):
            forward_qd(half, s, 1 - core).wait_recv()

    def receive_kv(half):
        for d in [0] + around:
            wait_from(functools.partial(copy_kv, half), d)

    def round_dkv(half):
        def one(s, carry):
            outs[half, 0, s] = (dkv[half, 0, s] * scale).astype(BF16)
            outs[half, 1, s] = dkv[half, 1, s].astype(BF16)
            return carry

        lax.fori_loop(0, chips, one, 0)

    def round_dq(half):
        def one(s, carry):
            outs[half, 2, s] = ((dqt[half, s, core] + dqx[half, s]) * scale).astype(BF16).T
            return carry

        lax.fori_loop(0, chips, one, 0)

    receive_qd(LATE)
    for d in [0] + around:
        wait_from(copy_ld, d)
        forward_ld((z - d + chips) % chips, core).start()
    receive_kv(LATE)
    receive_forwarded(LATE)
    for s in range(chips):
        forward_ld(s, 1 - core).wait_recv()
    sweep(LATE, LATE, lambda i: 0, lambda i: 2 * i + 2, 2, True)
    round_dkv(LATE)
    start_all(functools.partial(copy_dkv, LATE))

    receive_kv(EARLY)
    sweep(EARLY, LATE, lambda i: 0, lambda i: chips // 2, 4, False)
    exchange_dq(LATE).start()
    receive_qd(EARLY)
    exchange_dq(LATE).wait()
    round_dq(LATE)
    start_all(functools.partial(copy_dq, LATE))

    receive_forwarded(EARLY)
    sweep(EARLY, EARLY, lambda i: 2 * i, lambda i: chips, 2, True)
    round_dkv(EARLY)
    exchange_dq(EARLY).start()
    start_all(functools.partial(copy_dkv, EARLY))
    exchange_dq(EARLY).wait()
    round_dq(EARLY)
    start_all(functools.partial(copy_dq, EARLY))

    out = {0: dk_h, 1: dv_h, 2: dq_h}

    def store(t, half):
        rows = pl.ds(half * c, c)
        return pltpu.make_async_copy(outv.at[t, rows], out[t].at[rows], store_sem.at[t, half])

    def deliver(t, half):
        for h in range(heads):
            for l in range(dim // lanes):
                wide[l, head_rows(h), :] = outr[half, t, h, :, pl.ds(l * lanes, lanes)].astype(F32)
        for l in range(dim // lanes):
            outv[t, pl.ds(half * c, c), :, pl.ds(l * lanes, lanes)] = wide[l].reshape(c, heads, lanes).astype(BF16)
        store(t, half).start()

    for half in (LATE, EARLY):
        for d in [0] + around[::-1]:
            wait_from(functools.partial(copy_dkv, half), d)
        deliver(0, half)
        deliver(1, half)
        for d in [0] + around[::-1]:
            wait_from(functools.partial(copy_dq, half), d)
        deliver(2, half)

    for half in (LATE, EARLY):
        for make in (copy_kv, copy_qd, copy_dkv, copy_dq):
            wait_sent(functools.partial(make, half))
        for s in range(chips):
            forward_qd(half, s, core).wait_send()
        for t in range(3):
            store(t, half).wait()
    wait_sent(copy_ld)
    for s in range(chips):
        forward_ld(s, core).wait_send()


def solution(mesh):
    n = mesh.shape['cp']
    spec = P('data', 'cp', None, None)
    lspec = P('data', None, 'cp')

    def local(q, k, v, o, lse, do):
        batch, tokens, heads, dim = q.shape
        chips = n // 2
        assert batch == 1 and heads == chips
        c = tokens // 2
        dma = pltpu.SemaphoreType.DMA
        args = [x.reshape(tokens, heads, dim) for x in (q, k, v, o, do)] + [lse.reshape(heads, tokens)]
        outs = pl.pallas_call(
            functools.partial(_kernel, n),
            out_shape=[jax.ShapeDtypeStruct((tokens, heads, dim), BF16)] * 3,
            in_specs=[pl.BlockSpec(memory_space=pl.ANY)] * 6,
            out_specs=[pl.BlockSpec(memory_space=pl.ANY)] * 3,
            scratch_shapes=[
                pltpu.VMEM((5, tokens, heads, dim), BF16),
                pltpu.VMEM((heads, tokens), F32),
                pltpu.VMEM((dim // 128, c * heads, 128), F32),
                pltpu.VMEM((2, 4, heads, c, dim), BF16),
                pltpu.VMEM((heads, 4, c), F32),
                pltpu.VMEM((2, 2, chips, c, dim), BF16),
                pltpu.VMEM((2, 2, n, c, dim), BF16),
                pltpu.VMEM((n, 4, c), F32),
                pltpu.VMEM((dim, 2 * c), BF16),
                pltpu.VMEM((2, chips, 2, dim, c), F32),
                pltpu.VMEM((2, chips, dim, c), F32),
                pltpu.VMEM((2, 2, chips, c, dim), F32),
                pltpu.VMEM((2, 3, chips, c, dim), BF16),
                pltpu.VMEM((2, 3, heads, c, dim), BF16),
                pltpu.VMEM((3, tokens, heads, dim), BF16),
                dma((5, 2)), dma, dma((3, 2)),
                dma((2, chips)), dma((2, chips)), dma((2, chips)), dma((2, chips)), dma((chips,)), dma((chips,)),
                dma((2, chips)), dma((2, chips)), dma((chips,)), dma((chips,)), dma((2,)), dma((2,)),
                dma((2, chips)), dma((2, chips)), dma((2, chips)), dma((2, chips)),
            ],
            compiler_params=pltpu.CompilerParams(collective_id=0, has_side_effects=True,
                                                 vmem_limit_bytes=60 * 1024 * 1024),
            name='attention_backward',
        )(*args)
        dk, dv, dq = outs[1], outs[2], outs[0]
        return tuple(x.reshape(batch, tokens, heads, dim) for x in (dq, dk, dv))

    return jax.shard_map(local, mesh=mesh, in_specs=(spec, spec, spec, spec, lspec, spec),
                         out_specs=(spec, spec, spec), check_vma=False)
```

time: 1000 us -> 178 us (0.18); the launches traced: 989 us -> 178 us
  waiting for transfers between devices: 708 us -> 0 us
  Pallas kernels: 0 us -> 173 us
  matrix products: 121 us -> 0 us
  other arithmetic: 80 us -> 0 us
  local copies, waits for them, and re-layouts: 69 us -> 4.93 us
    ppermute x76 -> x0, waiting for transfers between devices: 708 us -> none  [the longest x75 705 us: local(): lax.ppermute(x, 'cp', nxt)]
    pallas_call x0 -> x1, Pallas kernels: none -> 173 us  [local(): pl.pallas_call(functools.partial(_kernel, n), out_shape=[jax.ShapeDtypeSt...]
    dot_general x85 -> x0, matrix products: 121 us -> none  [the longest x17 29.4 us: _pair(): jnp.einsum('bhqk,bqhd->bkhd', ds, q, preferred_element_type=F32) * scale]
    add x15 -> x0, other arithmetic: 56 us -> none  [local(): dq = dq + ddq]
    concatenate x31 -> x0, local copies, waits for them, and re-layouts: 44.8 us -> none  [the longest x15 23 us: _first_keys(): jnp.concatenate([dk, jnp.zeros_like(dk)], axis=1)]
    convert_element_type x2 -> x0, other arithmetic: 22.1 us -> none  [local(): return (dq.astype(BF16), dk.astype(BF16), dv.astype(BF16))]
    unnamed x46 -> x7, local copies, waits for them, and re-layouts: 17.1 us -> 4.93 us
  transfers between devices with their start and end apart: 76 -> 0, of which waited for: 31 -> 0; matrix products, arithmetic and copies ran while one was open for 20% -> 0% of each run, Pallas kernels for 0% -> 0%
where the time goes in v1:
time: 178 us
  Pallas kernels  173 us (97%)
  local copies, waits for them, and re-layouts  4.93 us (3%)
    pallas_call x1, Pallas kernels, local(): pl.pallas_call(functools.partial(_kernel, n), out_shape=[jax.ShapeDtypeSt...  173 us
    unnamed x7, local copies, waits for them, and re-layouts  4.93 us

profile of v1, /device:TPU:22, one launch (start us, length us, event | category | flops | bytes accessed | tf_op | source)
XLA Modules:
  0.0 178.2 jit_solution(5210671883420493982)
XLA Ops:
  0.6 172.7 %attention_backward.1 = (bf16[256,8,256]{2,1,0:T(8,128)(2,1)}, bf16[256,8,256]{2,1,0:T(8,128)(2,1)}, bf16[256,8,256]{2,1,0:T(8,128)(2,1)}) custom-call(bf16[256,8,256]{2,1,0:T(8,128)(2,1)} %bitcast.9, bf16[256,8,256]{2,1,0:T(8,128)(2,1)} %bitcast.10, bf16[256,8,256]{2,1,0:T(8,128)(2,1)} %bitcast.11, bf16[256,8,256]{2,1,0:T(8,128)(2,1)} %bitcast.12, ...), custom_call_target="tpu_custom_call" | custom-call | tf_op jit(solution)/shard_map/attention_backward/pallas_call | solution.py:321
  173.3 0.0 copy-start.1
  173.3 2.4 %copy.12 = bf16[1,256,8,256]{3,2,1,0:T(8,128)(2,1)} copy(bf16[1,256,8,256]{3,2,1,0:T(8,128)(2,1)} %bitcast.16) | data formatting | bytes 2097152
  175.7 0.0 copy-done.1
  175.7 0.0 copy-start
  175.7 1.0 copy.13
  176.6 0.6 copy-done
  177.3 1.0 copy.14
Async XLA Ops:
  173.3 2.4 %copy-start.1 = (bf16[256,8,256]{2,1,0:T(8,128)(2,1)S(1)}, bf16[256,8,256]{2,1,0:T(8,128)(2,1)}, u32[]{:S(2)}) copy-start(bf16[256,8,256]{2,1,0:T(8,128)(2,1)} %get-tuple-element.7) | copy-start | bytes 3145732
  175.7 1.6 copy-start

commit v2 on v1

--- a/solution.py
+++ b/solution.py
@@ -22,9 +22,9 @@
     return lax.dot_general(a, b, (((1,), (1,)), ((), ())), preferred_element_type=F32)
 
 
-def _kernel(n, q_h, k_h, v_h, o_h, do_h, lse_h, dq_h, dk_h, dv_h,
-            raw, lse_v, wide, send, ldsend, kv, qd, ld, kt, dqt, dqx, dkv, outs, outr, outv,
-            load_sem, lse_sem, store_sem, kv_s, kv_r, qd_s, qd_r, ld_s, ld_r,
+def _kernel(n, q_h, k_h, v_h, o_h, do_h, lse_h, outv,
+            raw, lse_v, wide, send, ldsend, kv, qd, ld, kt, dqt, dqx, dkv, outs, outr,
+            tokens_up, tokens_down, load_sem, lse_sem, kv_s, kv_r, qd_s, qd_r, ld_s, ld_r,
             fw_s, fw_r, fl_s, fl_r, dx_s, dx_r, og_s, og_r, oq_s, oq_r):
     chips = n // 2
     tokens, heads, dim = raw.shape[1:]
@@ -42,8 +42,9 @@
         return {'cp': 2 * chip + core}
 
     barrier = pltpu.get_barrier_semaphore()
-    for d in range(1, chips):
-        pl.semaphore_signal(barrier, inc=1, device_id=peer((z + d) % chips), device_id_type=MESH)
+    above, below = peer((z + 1) % chips), peer((z + chips - 1) % chips)
+    for near in (above, below):
+        pl.semaphore_signal(barrier, inc=1, device_id=near, device_id_type=MESH)
     pl.semaphore_signal(barrier, inc=1, device_id={'cp': sib}, device_id_type=MESH)
 
     hbm = {K: k_h, V: v_h, Q: q_h, DO: do_h, O: o_h}
@@ -52,15 +53,30 @@
         rows = pl.ds(half * c, c)
         return pltpu.make_async_copy(hbm[t].at[rows], raw.at[t, rows], load_sem.at[t, half])
 
-    for half in (LATE, EARLY):
-        for t in (K, V, Q, DO, O):
-            load(t, half).start()
+    load(K, LATE).start()
+    load(V, LATE).start()
+
+    pl.semaphore_wait(barrier, 3)
+
+    def pass_on(k):
+        pl.semaphore_signal(tokens_up.at[k], inc=1, device_id=above, device_id_type=MESH)
+        pl.semaphore_signal(tokens_down.at[k], inc=1, device_id=below, device_id_type=MESH)
+
+    def hear(k):
+        pl.semaphore_wait(tokens_up.at[k], 1)
+        pl.semaphore_wait(tokens_down.at[k], 1)
+
+    pass_on(1)
+    for t in (Q, DO, O):
+        load(t, LATE).start()
+    for t in (K, V, Q, DO, O):
+        load(t, EARLY).start()
     lse_load = pltpu.make_async_copy(lse_h, lse_v, lse_sem)
     lse_load.start()
 
     def spread(x):
         for l in range(dim // lanes):
-            wide[l] = x[:, :, l * lanes:(l + 1) * lanes].reshape(c * heads, lanes)
+            wide[0, l] = x[:, :, l * lanes:(l + 1) * lanes].reshape(c * heads, lanes)
 
     def head_rows(h):
         return pl.ds(h, c, stride=heads)
@@ -71,7 +87,7 @@
         spread(raw[t, pl.ds(half * c, c)].astype(F32))
         for h in range(heads):
             for l in range(dim // lanes):
-                send[half, t, h, :, pl.ds(l * lanes, lanes)] = wide[l, head_rows(h), :].astype(BF16)
+                send[half, t, h, :, pl.ds(l * lanes, lanes)] = wide[0, l, head_rows(h), :].astype(BF16)
 
     def copy_kv(half, d, slot):
         head = (z + d) % chips
@@ -143,8 +159,15 @@
 
     relayout(K, LATE)
     relayout(V, LATE)
-    pl.semaphore_wait(barrier, chips)
-    start_all(functools.partial(copy_kv, LATE))
+    copy_kv(LATE, 0, z).start()
+    for k in range(1, chips // 2 + 1):
+        if k > 1:
+            hear(k - 1)
+            if k < chips // 2:
+                pass_on(k)
+        for d in around[::-1]:
+            if min(d, chips - d) == k:
+                copy_kv(LATE, d, z).start()
     relayout(Q, LATE)
     relayout(DO, LATE)
     start_all(functools.partial(copy_qd, LATE))
@@ -156,7 +179,7 @@
         rows = pl.ds(half * c, c)
         spread(raw[DO, rows].astype(F32) * raw[O, rows].astype(F32))
         for h in range(heads):
-            prod = sum(wide[l, head_rows(h), :] for l in range(dim // lanes))
+            prod = sum(wide[0, l, head_rows(h), :] for l in range(dim // lanes))
             ldsend[h, pl.ds(2 + half, 1), :] = jnp.sum(prod.T, axis=0, keepdims=True)
             ldsend[h, pl.ds(half, 1), :] = lse_v[pl.ds(h, 1), pl.ds(half * c, c)]
     start_all(copy_ld)
@@ -271,39 +294,38 @@
     round_dq(EARLY)
     start_all(functools.partial(copy_dq, EARLY))
 
-    out = {0: dk_h, 1: dv_h, 2: dq_h}
-
-    def store(t, half):
-        rows = pl.ds(half * c, c)
-        return pltpu.make_async_copy(outv.at[t, rows], out[t].at[rows], store_sem.at[t, half])
-
-    def deliver(t, half):
-        for h in range(heads):
+    def gather(make, half, ts):
+        for d in [0] + around:
+            wait_from(functools.partial(make, half), d)
+            h = (z - d + chips) % chips
+            for t in ts:
+                for l in range(dim // lanes):
+                    wide[t, l, head_rows(h), :] = outr[half, t, h, :, pl.ds(l * lanes, lanes)].astype(F32)
+        for t in ts:
             for l in range(dim // lanes):
-                wide[l, head_rows(h), :] = outr[half, t, h, :, pl.ds(l * lanes, lanes)].astype(F32)
-        for l in range(dim // lanes):
-            outv[t, pl.ds(half * c, c), :, pl.ds(l * lanes, lanes)] = wide[l].reshape(c, heads, lanes).astype(BF16)
-        store(t, half).start()
+                outv[t, pl.ds(half * c, c), :, pl.ds(l * lanes, lanes)] = (
+                    wide[t, l].reshape(c, heads, lanes).astype(BF16))
 
     for half in (LATE, EARLY):
-        for d in [0] + around[::-1]:
-            wait_from(functools.partial(copy_dkv, half), d)
-        deliver(0, half)
-        deliver(1, half)
-        for d in [0] + around[::-1]:
-            wait_from(functools.partial(copy_dq, half), d)
-        deliver(2, half)
+        gather(copy_dkv, half, (0, 1))
+        gather(copy_dq, half, (2,))
 
     for half in (LATE, EARLY):
         for make in (copy_kv, copy_qd, copy_dkv, copy_dq):
             wait_sent(functools.partial(make, half))
         for s in range(chips):
             forward_qd(half, s, core).wait_send()
-        for t in range(3):
-            store(t, half).wait()
     wait_sent(copy_ld)
     for s in range(chips):
         forward_ld(s, core).wait_send()
+
+
+def _write(x, dk, dv, dq, sem):
+    copies = [pltpu.make_async_copy(x.at[t], out, sem.at[t]) for t, out in enumerate((dk, dv, dq))]
+    for copy in copies:
+        copy.start()
+    for copy in copies:
+        copy.wait()
 
 
 def solution(mesh):
@@ -318,15 +340,15 @@
         c = tokens // 2
         dma = pltpu.SemaphoreType.DMA
         args = [x.reshape(tokens, heads, dim) for x in (q, k, v, o, do)] + [lse.reshape(heads, tokens)]
-        outs = pl.pallas_call(
+        grads = pl.pallas_call(
             functools.partial(_kernel, n),
-            out_shape=[jax.ShapeDtypeStruct((tokens, heads, dim), BF16)] * 3,
+            out_shape=pltpu.VMEM((3, tokens, heads, dim), BF16),
             in_specs=[pl.BlockSpec(memory_space=pl.ANY)] * 6,
-            out_specs=[pl.BlockSpec(memory_space=pl.ANY)] * 3,
+            out_specs=pl.BlockSpec(memory_space=pltpu.VMEM),
             scratch_shapes=[
                 pltpu.VMEM((5, tokens, heads, dim), BF16),
                 pltpu.VMEM((heads, tokens), F32),
-                pltpu.VMEM((dim // 128, c * heads, 128), F32),
+                pltpu.VMEM((3, dim // 128, c * heads, 128), F32),
                 pltpu.VMEM((2, 4, heads, c, dim), BF16),
                 pltpu.VMEM((heads, 4, c), F32),
                 pltpu.VMEM((2, 2, chips, c, dim), BF16),
@@ -338,17 +360,25 @@
                 pltpu.VMEM((2, 2, chips, c, dim), F32),
                 pltpu.VMEM((2, 3, chips, c, dim), BF16),
                 pltpu.VMEM((2, 3, heads, c, dim), BF16),
-                pltpu.VMEM((3, tokens, heads, dim), BF16),
-                dma((5, 2)), dma, dma((3, 2)),
+                pltpu.SemaphoreType.REGULAR((chips // 2,)), pltpu.SemaphoreType.REGULAR((chips // 2,)),
+                dma((5, 2)), dma,
                 dma((2, chips)), dma((2, chips)), dma((2, chips)), dma((2, chips)), dma((chips,)), dma((chips,)),
                 dma((2, chips)), dma((2, chips)), dma((chips,)), dma((chips,)), dma((2,)), dma((2,)),
                 dma((2, chips)), dma((2, chips)), dma((2, chips)), dma((2, chips)),
             ],
             compiler_params=pltpu.CompilerParams(collective_id=0, has_side_effects=True,
-                                                 vmem_limit_bytes=60 * 1024 * 1024),
+                                                 vmem_limit_bytes=56 * 1024 * 1024),
             name='attention_backward',
         )(*args)
-        dk, dv, dq = outs[1], outs[2], outs[0]
+        dk, dv, dq = pl.pallas_call(
+            _write,
+            out_shape=[jax.ShapeDtypeStruct((tokens, heads, dim), BF16)] * 3,
+            in_specs=[pl.BlockSpec(memory_space=pltpu.VMEM)],
+            out_specs=[pl.BlockSpec(memory_space=pl.ANY)] * 3,
+            scratch_shapes=[dma((3,))],
+            compiler_params=pltpu.CompilerParams(vmem_limit_bytes=8 * 1024 * 1024),
+            name='write_gradients',
+        )(pltpu.with_memory_space_constraint(grads, pltpu.VMEM))
         return tuple(x.reshape(batch, tokens, heads, dim) for x in (dq, dk, dv))
 
     return jax.shard_map(local, mesh=mesh, in_specs=(spec, spec, spec, spec, lspec, spec),

time: 178 us -> 173 us (0.972)
  local copies, waits for them, and re-layouts: 4.93 us -> 0 us
    unnamed x7 -> x0, local copies, waits for them, and re-layouts: 4.93 us -> none
    pallas_call x1 -> x2, Pallas kernels: 173 us -> 172 us  [the longest x1 171 us: local(): pl.pallas_call(functools.partial(_kernel, n), out_shape=pltpu.VMEM((3, to...]
where the time goes in v2:
time: 173 us
  Pallas kernels  172 us (99%)
    pallas_call x1, Pallas kernels, local(): pl.pallas_call(functools.partial(_kernel, n), out_shape=pltpu.VMEM((3, to...  171 us

profile of v2, /device:TPU:22, one launch (start us, length us, event | category | flops | bytes accessed | tf_op | source)
XLA Modules:
  0.0 173.1 jit_solution(3771317975737880179)
XLA Ops:
  0.6 170.8 %attention_backward.1.x = bf16[3,256,8,256]{3,2,1,0:T(8,128)(2,1)S(1)} custom-call(bf16[256,8,256]{2,1,0:T(8,128)(2,1)} %bitcast.9, bf16[256,8,256]{2,1,0:T(8,128)(2,1)} %bitcast.10, bf16[256,8,256]{2,1,0:T(8,128)(2,1)} %bitcast.11, bf16[256,8,256]{2,1,0:T(8,128)(2,1)} %bitcast.12, bf16[256,8,256]{2,1,0:T(8,128)(2,1)} %bitcast.13, f32[8,256]{1,0:T(8,128)} %bitcast.14), custom_call_target="tpu_custom_call" | custom-call | tf_op jit(solution)/shard_map/attention_backward/pallas_call | solution.py:343
  171.4 1.7 write_gradients.1

commit v3 on v2

--- a/solution.py
+++ b/solution.py
@@ -35,8 +35,7 @@
     z = me // 2
     core = me % 2
     sib = me + 1 - 2 * core
-    around = list(range(chips // 2, 0, -1))
-    around = [d for k in around for d in ([k] if 2 * k == chips else [k, chips - k])]
+    around = [d for k in range(1, chips // 2) for d in (k, chips - k)] + [chips // 2]
 
     def peer(chip):
         return {'cp': 2 * chip + core}
@@ -92,7 +91,7 @@
     def copy_kv(half, d, slot):
         head = (z + d) % chips
         src, dst = send.at[half, pl.ds(K, 2), head], kv.at[half, :, slot]
-        if d == 0:
+        if isinstance(d, int) and d == 0:
             return pltpu.make_async_copy(src, dst, kv_r.at[half, slot])
         return pltpu.make_async_remote_copy(src, dst, kv_s.at[half, d], kv_r.at[half, slot],
                                             device_id=peer(head), device_id_type=MESH)
@@ -100,7 +99,7 @@
     def copy_qd(half, d, slot):
         head = (z + d) % chips
         src, dst = send.at[half, pl.ds(Q, 2), head], qd.at[half, :, 2 * slot + core]
-        if d == 0:
+        if isinstance(d, int) and d == 0:
             return pltpu.make_async_copy(src, dst, qd_r.at[half, slot])
         return pltpu.make_async_remote_copy(src, dst, qd_s.at[half, d], qd_r.at[half, slot],
                                             device_id=peer(head), device_id_type=MESH)
@@ -108,7 +107,7 @@
     def copy_ld(d, slot):
         head = (z + d) % chips
         src, dst = ldsend.at[head], ld.at[2 * slot + core]
-        if d == 0:
+        if isinstance(d, int) and d == 0:
             return pltpu.make_async_copy(src, dst, ld_r.at[slot])
         return pltpu.make_async_remote_copy(src, dst, ld_s.at[d], ld_r.at[slot],
                                             device_id=peer(head), device_id_type=MESH)
@@ -130,7 +129,7 @@
     def copy_dkv(half, d, slot):
         chip = (z + d) % chips
         src, dst = outs.at[half, pl.ds(0, 2), chip], outr.at[half, pl.ds(0, 2), slot]
-        if d == 0:
+        if isinstance(d, int) and d == 0:
             return pltpu.make_async_copy(src, dst, og_r.at[half, slot])
         return pltpu.make_async_remote_copy(src, dst, og_s.at[half, d], og_r.at[half, slot],
                                             device_id=peer(chip), device_id_type=MESH)
@@ -138,14 +137,28 @@
     def copy_dq(half, d, slot):
         chip = (z + d) % chips
         src, dst = outs.at[half, 2, chip], outr.at[half, 2, slot]
-        if d == 0:
+        if isinstance(d, int) and d == 0:
             return pltpu.make_async_copy(src, dst, oq_r.at[half, slot])
         return pltpu.make_async_remote_copy(src, dst, oq_s.at[half, d], oq_r.at[half, slot],
                                             device_id=peer(chip), device_id_type=MESH)
 
     def start_all(make):
-        for d in around + [0]:
+        for d in [0] + around:
             make(d, z).start()
+
+    def start_all_low_first(make):
+        @pl.when(z == 0)
+        def _():
+            make(0, z).start()
+
+        @pl.when(z != 0)
+        def _():
+            make(chips - z, z).start()
+
+        for d in [0] + around:
+            @pl.when((z + d) % chips != 0)
+            def _():
+                make(d, z).start()
 
     def wait_from(make, d):
         if d == 0:
@@ -165,7 +178,7 @@
             hear(k - 1)
             if k < chips // 2:
                 pass_on(k)
-        for d in around[::-1]:
+        for d in around:
             if min(d, chips - d) == k:
                 copy_kv(LATE, d, z).start()
     relayout(Q, LATE)
@@ -238,7 +251,7 @@
         lax.fori_loop(0, chips // 2, outer, 0)
 
     def receive_qd(half):
-        for d in [0] + around[::-1]:
+        for d in [0] + around:
             wait_from(functools.partial(copy_qd, half), d)
             forward_qd(half, (z - d + chips) % chips, core).start()
 
@@ -292,7 +305,7 @@
     start_all(functools.partial(copy_dkv, EARLY))
     exchange_dq(EARLY).wait()
     round_dq(EARLY)
-    start_all(functools.partial(copy_dq, EARLY))
+    start_all_low_first(functools.partial(copy_dq, EARLY))
 
     def gather(make, half, ts):
         for d in [0] + around:

time: 173 us -> 171 us (0.988)
  Pallas kernels: 172 us -> 170 us
    pallas_call x1, Pallas kernels: 171 us -> 169 us  [local(): pl.pallas_call(functools.partial(_kernel, n), out_shape=pltpu.VMEM((3, to...]
where the time goes in v3:
time: 171 us
  Pallas kernels  170 us (99%)
    pallas_call x1, Pallas kernels, local(): pl.pallas_call(functools.partial(_kernel, n), out_shape=pltpu.VMEM((3, to...  169 us

profile of v3, /device:TPU:22, one launch (start us, length us, event | category | flops | bytes accessed | tf_op | source)
XLA Modules:
  0.0 171.0 jit_solution(14753360730057859315)
XLA Ops:
  0.6 168.7 %attention_backward.1.x = bf16[3,256,8,256]{3,2,1,0:T(8,128)(2,1)S(1)} custom-call(bf16[256,8,256]{2,1,0:T(8,128)(2,1)} %bitcast.9, bf16[256,8,256]{2,1,0:T(8,128)(2,1)} %bitcast.10, bf16[256,8,256]{2,1,0:T(8,128)(2,1)} %bitcast.11, bf16[256,8,256]{2,1,0:T(8,128)(2,1)} %bitcast.12, bf16[256,8,256]{2,1,0:T(8,128)(2,1)} %bitcast.13, f32[8,256]{1,0:T(8,128)} %bitcast.14), custom_call_target="tpu_custom_call" | custom-call | tf_op jit(solution)/shard_map/attention_backward/pallas_call | solution.py:356
  169.3 1.7 write_gradients.1

commit v4 on v3

--- a/solution.py
+++ b/solution.py
@@ -35,7 +35,7 @@
     z = me // 2
     core = me % 2
     sib = me + 1 - 2 * core
-    around = [d for k in range(1, chips // 2) for d in (k, chips - k)] + [chips // 2]
+    around = [d for k in range(1, chips // 2) for d in (chips - k, k)] + [chips // 2]
 
     def peer(chip):
         return {'cp': 2 * chip + core}

time: 171 us -> 171 us (level)
  no operation moved by 1% of the time
where the time goes in v4:
time: 171 us
  Pallas kernels  170 us (99%)
    pallas_call x1, Pallas kernels, local(): pl.pallas_call(functools.partial(_kernel, n), out_shape=pltpu.VMEM((3, to...  168 us

profile of v4, /device:TPU:22, one launch (start us, length us, event | category | flops | bytes accessed | tf_op | source)
XLA Modules:
  0.0 170.5 jit_solution(6903291855263762113)
XLA Ops:
  0.6 168.2 %attention_backward.1.x = bf16[3,256,8,256]{3,2,1,0:T(8,128)(2,1)S(1)} custom-call(bf16[256,8,256]{2,1,0:T(8,128)(2,1)} %bitcast.9, bf16[256,8,256]{2,1,0:T(8,128)(2,1)} %bitcast.10, bf16[256,8,256]{2,1,0:T(8,128)(2,1)} %bitcast.11, bf16[256,8,256]{2,1,0:T(8,128)(2,1)} %bitcast.12, bf16[256,8,256]{2,1,0:T(8,128)(2,1)} %bitcast.13, f32[8,256]{1,0:T(8,128)} %bitcast.14), custom_call_target="tpu_custom_call" | custom-call | tf_op jit(solution)/shard_map/attention_backward/pallas_call | solution.py:356
  168.9 1.7 write_gradients.1

commit v5 on v4

--- a/solution.py
+++ b/solution.py
@@ -302,13 +302,13 @@
     sweep(EARLY, EARLY, lambda i: 2 * i, lambda i: chips, 2, True)
     round_dkv(EARLY)
     exchange_dq(EARLY).start()
-    start_all(functools.partial(copy_dkv, EARLY))
+    start_all_low_first(functools.partial(copy_dkv, EARLY))
     exchange_dq(EARLY).wait()
     round_dq(EARLY)
     start_all_low_first(functools.partial(copy_dq, EARLY))
 
     def gather(make, half, ts):
-        for d in [0] + around:
+        for d in [0] + around[::-1]:
             wait_from(functools.partial(make, half), d)
             h = (z - d + chips) % chips
             for t in ts:

time: 171 us -> 171 us (level)
  no operation moved by 1% of the time
where the time goes in v5:
time: 171 us
  Pallas kernels  170 us (99%)
    pallas_call x1, Pallas kernels, local(): pl.pallas_call(functools.partial(_kernel, n), out_shape=pltpu.VMEM((3, to...  168 us

profile of v5, /device:TPU:22, one launch (start us, length us, event | category | flops | bytes accessed | tf_op | source)
XLA Modules:
  0.0 170.6 jit_solution(12865560289075517930)
XLA Ops:
  0.6 168.3 %attention_backward.1.x = bf16[3,256,8,256]{3,2,1,0:T(8,128)(2,1)S(1)} custom-call(bf16[256,8,256]{2,1,0:T(8,128)(2,1)} %bitcast.9, bf16[256,8,256]{2,1,0:T(8,128)(2,1)} %bitcast.10, bf16[256,8,256]{2,1,0:T(8,128)(2,1)} %bitcast.11, bf16[256,8,256]{2,1,0:T(8,128)(2,1)} %bitcast.12, bf16[256,8,256]{2,1,0:T(8,128)(2,1)} %bitcast.13, f32[8,256]{1,0:T(8,128)} %bitcast.14), custom_call_target="tpu_custom_call" | custom-call | tf_op jit(solution)/shard_map/attention_backward/pallas_call | solution.py:356
  168.9 1.7 write_gradients.1
